TPU v7x, 256 devices: a 4x2x16 block of a 4x16x16 slice. The times are simulated.
256 devices in a mesh: parts: 2 (over y), dp: 64 (over x, z), tensor: 2 (over core).
Axes of the slice: x: 4, y: 2, z: 16, core: 2. Of those that a mesh axis runs over, the one named last changes fastest.
The devices are a block of a 4x16x16 slice.
Arguments:
- normed: bfloat16 [128, 256, 4096], P(('parts', 'dp')), parts along dimension 0, may hold values from -28 to 28
- q_weight: bfloat16 [4096, 2048], P('dp', 'tensor'), may hold values from -0.09375 to 0.09375
- kv_weight: bfloat16 [4096, 2, 512], P('dp', None, 'tensor'), may hold values from -0.09375 to 0.09375
- o_weight: bfloat16 [2048, 4096], P('tensor', 'dp'), may hold values from -0.5 to 0.5
- lengths: int32 [128], P(('parts', 'dp')), parts along dimension 0, may hold values from 64 to 256
- destinations: int32 [128], P(('parts', 'dp')), parts along dimension 0, may hold values from 0 to 63, each once
Outputs:
- projected: bfloat16 [128, 256, 4096], P(('parts', 'dp'), None, 'tensor'), parts along dimension 0
- kv_cache: bfloat16 [128, 2, 4, 256, 128], P(('parts', 'dp'), None, None, 'tensor'), parts along dimension 0
There are 2 independent parts, one for each index of `parts`. A program takes and returns all parts, laid end to end along the dimension named above; an argument that names none is the same for every part. Nothing has to cross between parts.
All inputs are finite; a program needn't handle non-finite values.
Results may differ from a plain program's by a relative error of at most 0.012.
The roundings to bfloat16 on the way count: a program that leaves them out, or rounds other values in their place, can miss the bound.
Values may be sent and summed in bfloat16 or wider, within the bound.
A program may use at most 128 MiB of HBM per device.

v0:
```python
import math

import jax
import jax.numpy as jnp
from jax import lax
from jax.sharding import PartitionSpec as P

HD = 128


ROPE_BASE = 500000.0


def copy_for_each(array, axis):
    copies = jnp.broadcast_to(array, (lax.axis_size(axis), *array.shape))
    return lax.all_to_all(copies, axis, split_axis=0, concat_axis=0, tiled=True)


def in_order(blocks, dim):
    blocks = jnp.moveaxis(blocks, 0, dim)
    lengths = blocks.shape
    return blocks.reshape(*lengths[:dim], lengths[dim] * lengths[dim + 1], *lengths[dim + 2 :])


def gather_directly(array, axis, dim):
    blocks = copy_for_each(array, axis)
    return in_order(blocks, dim)


def in_one_piece(arrays, axis, dim, along):
    widths = [math.prod(a.shape[along:]) for a in arrays]
    both = jnp.concatenate(
        [a.reshape(*a.shape[:along], w) for a, w in zip(arrays, widths)], axis=along
    )
    filled = lax.all_gather(both, axis, axis=dim, tiled=True)
    blocks = jnp.split(filled, [sum(widths[:k]) for k in range(1, len(widths))], axis=along)
    return tuple(
        (b.reshape(*filled.shape[:along], *a.shape[along:]) for a, b in zip(arrays, blocks))
    )


def in_blocks(array, dim, size):
    before, after = (array.shape[:dim], array.shape[dim + 1 :])
    return jnp.moveaxis(array.reshape(*before, size, -1, *after), dim, 0)


def summed_on_arrival(array, axis, dim):
    size = lax.axis_size(axis)
    blocks = lax.all_to_all(in_blocks(array, dim, size), axis, 0, 0, tiled=True)
    return jnp.sum(blocks, axis=0)


def rotate(values, positions):
    half = values.shape[-1] // 2
    steps = jnp.arange(half, dtype=jnp.float32) * (2.0 / values.shape[-1])
    freq = jnp.power(jnp.float32(ROPE_BASE), -steps)
    angle = positions.astype(jnp.float32)[:, None] * freq[None, :]
    cosine = jnp.cos(angle)[:, None, :]
    sine = jnp.sin(angle)[:, None, :]
    first = values[..., :half]
    second = values[..., half:]
    return jnp.concatenate(
        [first * cosine - second * sine, second * cosine + first * sine], axis=-1
    )


def attend(queries, keys, values, length):
    total = keys.shape[1]
    block = min(total, 512)
    count = total // block
    key_pos = jnp.arange(total, dtype=jnp.int32)

    def one_block(index):
        start = index * block
        scores = jnp.einsum(
            "kgqd,ktd->kgqt", queries, keys, preferred_element_type=jnp.float32
        ) / math.sqrt(HD)
        query_pos = start + jnp.arange(block, dtype=jnp.int32)
        allowed = (query_pos[:, None] >= key_pos[None, :]) & (key_pos[None, :] < length)
        scores = jnp.where(allowed, scores, -jnp.inf)
        peak = jnp.max(scores, axis=-1, keepdims=True)
        expo = jnp.exp(scores - peak)
        weights = (expo / jnp.sum(expo, axis=-1, keepdims=True)).astype(jnp.bfloat16)
        return jnp.einsum(
            "kgqt,ktd->kgqd", weights, values, preferred_element_type=jnp.float32
        ).astype(jnp.bfloat16)

    blocks = lax.map(one_block, jnp.arange(count, dtype=jnp.int32))
    return blocks.transpose(0, 3, 1, 2, 4).reshape(total, -1)


def regroup(cache):
    return lax.all_to_all(cache, "tensor", split_axis=2, concat_axis=1, tiled=True)


def deliver(cache, destination):
    count = lax.axis_size("dp")
    flat = cache.reshape(count, -1)
    sent_to = gather_directly(destination, "dp", 0)
    spread = lax.all_to_all(flat, "dp", split_axis=0, concat_axis=0, tiled=True)
    slots = jnp.arange(count, dtype=jnp.int32)
    match = sent_to[None, :] == slots[:, None]
    source = jnp.sum(jnp.where(match, slots[None, :], 0), axis=1)
    outgoing = jnp.take(spread, source, axis=0)
    arrived = lax.all_to_all(outgoing, "dp", split_axis=0, concat_axis=0, tiled=True)
    return arrived.reshape(cache.shape)


def on_device(normed, q_weight, kv_weight, o_weight, lengths, destinations):
    tokens = normed[0]
    total = tokens.shape[0]
    q_local = q_weight.shape[1] // HD
    kv_local = kv_weight.shape[2] // HD
    group = q_local // kv_local
    q_full, kv_full = in_one_piece((q_weight, kv_weight), "dp", 0, 1)
    query_raw = jnp.dot(tokens, q_full, preferred_element_type=jnp.float32)
    pair_raw = jnp.dot(
        tokens, kv_full.reshape(kv_full.shape[0], -1), preferred_element_type=jnp.float32
    )
    positions = jnp.arange(total, dtype=jnp.int32)
    query = rotate(query_raw.reshape(total, q_local, HD), positions).astype(jnp.bfloat16)
    pair = pair_raw.reshape(total, 2, kv_local, HD)
    keys = rotate(pair[:, 0], positions).astype(jnp.bfloat16)
    values = pair[:, 1].astype(jnp.bfloat16)
    grouped = query.reshape(total, kv_local, group, HD).transpose(1, 2, 0, 3)
    key_rows = keys.transpose(1, 0, 2)
    value_rows = values.transpose(1, 0, 2)
    length = lengths[0]
    attended = attend(grouped, key_rows, value_rows, length)
    partial_sums = jnp.dot(
        attended,
        lax.all_gather(o_weight, "dp", axis=1, tiled=True),
        preferred_element_type=jnp.float32,
    )
    projected = summed_on_arrival(partial_sums, "tensor", 1).astype(jnp.bfloat16)
    live = (positions < length)[None, :, None]
    kept_keys = jnp.where(live, key_rows, jnp.zeros_like(key_rows))
    kept_values = jnp.where(live, value_rows, jnp.zeros_like(value_rows))
    cache = jnp.stack([kept_keys, kept_values], axis=0)
    routed = deliver(regroup(cache), destinations)
    return (projected[None], routed[None])


def solution(mesh):
    placed = (
        P(("parts", "dp"), None, None),
        P("dp", "tensor"),
        P("dp", None, "tensor"),
        P("tensor", "dp"),
        P(("parts", "dp")),
        P(("parts", "dp")),
    )
    return jax.shard_map(
        on_device,
        mesh=mesh,
        in_specs=placed,
        out_specs=(
            P(("parts", "dp"), None, "tensor"),
            P(("parts", "dp"), None, None, "tensor", None),
        ),
        check_vma=False,
    )
```

profile of v0, /device:TPU:33, one launch (start us, length us, event | category | flops | bytes accessed | tf_op | source)
XLA Modules:
  0.0 401.7 jit_solution(113619744113657147)
XLA Ops:
  7.3 1.0 copy.79
  8.2 1.6 pad_maximum_fusion.1
  9.9 0.1 all-gather.5.cloned.1.call-start
  10.0 0.7 all-gather.5.cloned.1.call-update
  11.4 0.6 broadcast_in_dim.76
  12.0 29.6 %all-to-all-start.1 = ((s32[64,1,1]{2,1,0:T(1,128)}), s32[64,1,1]{2,1,0:T(1,128)S(1)}, u32[]{:S(2)}, u32[]{:S(2)}) async-start(s32[64,1,1]{2,1,0:T(1,128)} %broadcast_in_dim.76), calls=%async_computation.1 | async-start | bytes 65536 | tf_op jit(solution)/shard_map/all_to_all | solution.py:16
  42.3 0.3 multiply_cosine_fusion
  42.6 0.7 fusion.14
  43.3 0.7 copy.60
  44.0 0.7 copy.59
  44.8 8.7 %all-to-all-done.1 = s32[64,1,1]{2,1,0:T(1,128)S(1)} async-done(((s32[64,1,1]{2,1,0:T(1,128)}), s32[64,1,1]{2,1,0:T(1,128)S(1)}, u32[]{:S(2)}, u32[]{:S(2)}) %all-to-all-start.1) | async-done | bytes 288 | tf_op jit(solution)/shard_map/all_to_all | solution.py:16
  53.5 1.2 reduce
  54.7 0.1 select_reduce_fusion
  54.9 135.2 %all-gather.3.cloned.1.call-done = bf16[4096,1536]{1,0:T(8,128)(2,1)} async-done(((bf16[64,1536]{1,0:T(8,128)(2,1)}), bf16[4096,1536]{1,0:T(8,128)(2,1)}) %all-gather.3.cloned.1.call-update) | async-done | bytes 12582928 | tf_op jit(solution)/shard_map/all_gather | solution.py:35
  190.1 3.5 fusion.3
  193.6 5.8 %fusion.1 = f32[1024,256]{1,0:T(8,128)S(1)} fusion(bf16[4096,1536]{1,0:T(8,128)(2,1)} %all-gather.3.cloned.1.call-done, bf16[1,256,4096]{2,1,0:T(8,128)(2,1)S(1)} %copy-done), kind=kOutput, calls=%fused_computation.2 | convolution fusion | flops 2147483648 | bytes 11534336 | tf_op jit(solution)/shard_map/dot_general | solution.py:116
  199.4 0.2 subtract_convert_fusion
  199.6 0.3 copy.57
  199.8 1.0 copy.56
  200.8 0.1 copy.77
  201.0 0.1 copy.78
  201.1 1.2 subtract_convert_fusion.1
  202.3 0.1 fusion.22
  202.5 0.3 copy.65
  202.8 6.8 %all_to_all.45 = bf16[2,2,256,128]{3,1,0,2:T(2,128)(2,1)S(1)} all-to-all(bf16[2,2,256,128]{3,1,0,2:T(2,128)(2,1)S(1)} %copy.65), channel_id=1, replica_groups=mesh['parts'=2,'dp'=64,'tensor'=2] {'tensor'}, dimensions={2} | all-to-all | bytes 524288 | tf_op jit(solution)/shard_map/all_to_all | solution.py:93
  209.6 0.1 all_to_all.39
  209.7 0.5 broadcast.133
  210.3 2.1 reduce.2
  212.4 0.9 reshape.172
  213.3 10.5 %all-to-all-start.3 = ((bf16[64,2,1024]{2,1,0:T(2,128)(2,1)}), bf16[64,2,1024]{2,1,0:T(2,128)(2,1)S(1)}, u32[]{:S(2)}, u32[]{:S(2)}) async-start(bf16[64,2,1024]{2,1,0:T(2,128)(2,1)} %reshape.172), calls=%async_computation.3 | async-start | bytes 524288 | tf_op jit(solution)/shard_map/all_to_all | solution.py:100
  223.8 3.5 fusion.30
  227.3 1.9 convolution_convert_fusion
  229.3 107.8 %all-gather.5.cloned.1.call-done = bf16[1024,4096]{0,1:T(8,128)(2,1)} async-done(((bf16[1024,64]{0,1:T(8,128)(2,1)}), bf16[1024,4096]{0,1:T(8,128)(2,1)}) %all-gather.5.cloned.1.call-update) | async-done | bytes 8388624 | tf_op jit(solution)/shard_map/all_gather | solution.py:132
  337.1 7.7 %convolution_bitcast_fusion = f32[2,256,2048]{2,1,0:T(8,128)} fusion(bf16[256,1024,1]{0,1,2:T(8,128)(2,1)S(1)} %bitcast.109, bf16[2,2048,1024]{2,1,0:T(8,128)(2,1)} %bitcast.108), kind=kOutput, calls=%fused_computation.6 | convolution fusion | flops 2147483648 | bytes 13107200 | tf_op jit(solution)/shard_map/dot_general | solution.py:130
  344.8 14.6 %all-to-all-start = ((f32[2,256,2048]{2,1,0:T(8,128)}), f32[2,256,2048]{2,1,0:T(8,128)}, u32[]{:S(2)}, u32[]{:S(2)}) async-start(f32[2,256,2048]{2,1,0:T(8,128)} %convolution_bitcast_fusion), calls=%async_computation | async-start | bytes 8388608 | tf_op jit(solution)/shard_map/all_to_all | solution.py:49
  359.4 0.2 reshape.173
  359.6 0.2 copy.82
  359.8 0.7 gather_fusion
  360.5 0.1 bitcast_select_fusion
  360.6 0.7 reduce.3
  361.4 0.9 reshape.174
  362.2 1.3 all-to-all-done
  363.5 10.5 %all-to-all-start.4 = ((bf16[64,2,1024]{2,1,0:T(2,128)(2,1)}), bf16[64,2,1024]{2,1,0:T(2,128)(2,1)S(1)}, u32[]{:S(2)}, u32[]{:S(2)}) async-start(bf16[64,2,1024]{2,1,0:T(2,128)(2,1)} %reshape.174), calls=%async_computation.4 | async-start | bytes 524288 | tf_op jit(solution)/shard_map/all_to_all | solution.py:105
  374.0 3.8 reduce_sum.31
  377.8 14.4 %all-to-all-done.4 = bf16[64,2,1024]{2,1,0:T(2,128)(2,1)S(1)} async-done(((bf16[64,2,1024]{2,1,0:T(2,128)(2,1)}), bf16[64,2,1024]{2,1,0:T(2,128)(2,1)S(1)}, u32[]{:S(2)}, u32[]{:S(2)}) %all-to-all-start.4) | async-done | bytes 262176 | tf_op jit(solution)/shard_map/all_to_all | solution.py:105
  392.2 0.2 reshape.175
  392.5 1.5 reduce.1
  394.0 0.8 broadcast_in_dim_reshape.4
  (21 shorter events, 0.3 us)
Async XLA Ops:
  7.2 182.9 %copy-start = (bf16[1,256,4096]{2,1,0:T(8,128)(2,1)S(1)}, bf16[1,256,4096]{2,1,0:T(8,128)(2,1)}, u32[]{:S(2)}) copy-start(bf16[1,256,4096]{2,1,0:T(8,128)(2,1)} %param.6) | copy-start | bytes 6291460
  7.2 182.9 %all-gather.3.cloned.1.call-start = ((), (), s32[]{:S(2)}) async-start(), calls=%async_computation.5 | async-start | bytes 12779520 | tf_op jit(solution)/shard_map/all_gather | solution.py:35
  9.9 327.2 %all-gather.5.cloned.1.call-start = ((), (), s32[]{:S(2)}) async-start(), calls=%async_computation.6 | async-start | bytes 8519680 | tf_op jit(solution)/shard_map/all_gather | solution.py:132
  12.0 41.5 %all-to-all-start.1 = ((s32[64,1,1]{2,1,0:T(1,128)}), s32[64,1,1]{2,1,0:T(1,128)S(1)}, u32[]{:S(2)}, u32[]{:S(2)}) async-start(s32[64,1,1]{2,1,0:T(1,128)} %broadcast_in_dim.76), calls=%async_computation.1 | async-start | bytes 65536 | tf_op jit(solution)/shard_map/all_to_all | solution.py:16
  201.1 1.4 copy-start.1
  202.3 7.3 %copy-start.3 = (bf16[256,2,64]{2,0,1:T(8,128)(2,1)}, bf16[256,2,64]{2,0,1:T(8,128)(2,1)S(1)}, u32[]{:S(2)}) copy-start(bf16[256,2,64]{2,0,1:T(8,128)(2,1)S(1)} %get-tuple-element.19) | copy-start | bytes 196612
  213.3 131.5 %all-to-all-start.3 = ((bf16[64,2,1024]{2,1,0:T(2,128)(2,1)}), bf16[64,2,1024]{2,1,0:T(2,128)(2,1)S(1)}, u32[]{:S(2)}, u32[]{:S(2)}) async-start(bf16[64,2,1024]{2,1,0:T(2,128)(2,1)} %reshape.172), calls=%async_computation.3 | async-start | bytes 524288 | tf_op jit(solution)/shard_map/all_to_all | solution.py:100
  223.8 3.5 copy-start.2
  344.8 18.7 %all-to-all-start = ((f32[2,256,2048]{2,1,0:T(8,128)}), f32[2,256,2048]{2,1,0:T(8,128)}, u32[]{:S(2)}, u32[]{:S(2)}) async-start(f32[2,256,2048]{2,1,0:T(8,128)} %convolution_bitcast_fusion), calls=%async_computation | async-start | bytes 8388608 | tf_op jit(solution)/shard_map/all_to_all | solution.py:49
  363.5 28.7 %all-to-all-start.4 = ((bf16[64,2,1024]{2,1,0:T(2,128)(2,1)}), bf16[64,2,1024]{2,1,0:T(2,128)(2,1)S(1)}, u32[]{:S(2)}, u32[]{:S(2)}) async-start(bf16[64,2,1024]{2,1,0:T(2,128)(2,1)} %reshape.174), calls=%async_computation.4 | async-start | bytes 524288 | tf_op jit(solution)/shard_map/all_to_all | solution.py:105
Sparse Core Ops, SparseCore 0:
  11.0 179.0 all-gather.2
  192.5 144.5 all-gather.4
where the time goes:
time: 403 us; the launch traced here: 402 us
  waiting for transfers between devices  268 us (67%)
  starting transfers between devices  65.3 us (16%)
  matrix products  22.4 us (6%)
  between operations  15.6 us (4%)
  other arithmetic  13.7 us (3%)
  local copies, waits for them, and re-layouts  9.6 us (2%)
  blocking collectives  6.76 us (2%)
    all_gather x1, waiting for transfers between devices, in_one_piece(): filled = lax.all_gather(both, axis, axis=dim, tiled=True)  135 us
    all_gather x1, waiting for transfers between devices, on_device(): lax.all_gather(o_weight, 'dp', axis=1, tiled=True)  108 us
    all_to_all x1, starting transfers between devices, copy_for_each(): return lax.all_to_all(copies, axis, split_axis=0, concat_axis=0, tiled=True)  29.6 us
    all_to_all x1, starting transfers between devices, summed_on_arrival(): blocks = lax.all_to_all(in_blocks(array, dim, size), axis, 0, 0, tiled=True)  14.6 us
    all_to_all x1, waiting for transfers between devices, deliver(): lax.all_to_all(outgoing, 'dp', split_axis=0, concat_axis=0, tiled=True)  14.4 us
    all_to_all x1, starting transfers between devices, deliver(): spread = lax.all_to_all(flat, 'dp', split_axis=0, concat_axis=0, tiled=True)  10.5 us
    all_to_all x1, starting transfers between devices, deliver(): lax.all_to_all(outgoing, 'dp', split_axis=0, concat_axis=0, tiled=True)  10.5 us
    all_to_all x1, waiting for transfers between devices, copy_for_each(): return lax.all_to_all(copies, axis, split_axis=0, concat_axis=0, tiled=True)  8.7 us
  transfers between devices with their start and end apart: 6, of which 5 were waited for; matrix products, arithmetic and copies ran while one was open for 10% of the time, Pallas kernels for 0%

commit v1 on v0

v1 whole, which is shorter than its diff:
```python
import functools
import math

import jax
import jax.numpy as jnp
from jax import lax
from jax.experimental import pallas as pl
from jax.experimental.pallas import tpu as pltpu
from jax.sharding import PartitionSpec as P

HD = 128
ROPE_BASE = 500000.0
NX = 4
KC = 512
QC = 64


def tables(total):
    half = HD // 2
    steps = jnp.arange(half, dtype=jnp.float32) * (2.0 / HD)
    freq = jnp.power(jnp.float32(ROPE_BASE), -steps)
    angle = jnp.arange(total, dtype=jnp.float32)[:, None] * freq[None, :]
    cosine, sine = jnp.cos(angle), jnp.sin(angle)
    return (
        jnp.concatenate([cosine, cosine], axis=-1),
        jnp.concatenate([-sine, sine], axis=-1),
    )


def remote(src, dst, send, recv, device):
    return pltpu.make_async_remote_copy(
        src_ref=src,
        dst_ref=dst,
        send_sem=send,
        recv_sem=recv,
        device_id=device,
        device_id_type=pl.DeviceIdType.MESH,
    )


def kernel(
    nz, x_hbm, wcat, o_t, cos_ref, sin_ref, meta_ref, out_hbm, kv_hbm,
    wbuf, wobuf, xbuf, att, acc, oacc, obuf, meta, dests, srcv, srcs, kvall, swap, spread, perm, heads,
    meta_s, meta_r, w0_s, w0_r, ring_s, ring_r, sib_s, sib_r, y_s, y_r, ysib_s, ysib_r, own_s, own_r,
    o_s, o_r, osib_s, osib_r, oown_s, oown_r, x_l, x_s, xf_s, x_r, a_s, af_s, a_r, swap_s, swap_r,
    dest_s, dest_r, c1_s, c1_r, src_l, c2_s, c2_r, c3_s, c3_r, c3_l, out_s, out_r, out_l,
):
    part, dp, c = lax.axis_index("parts"), lax.axis_index("dp"), lax.axis_index("tensor")
    x, z = lax.div(dp, nz), lax.rem(dp, nz)
    half = nz // 2
    yb = lax.rem(part, 2)
    mate = part + 1 - 2 * yb
    rows = wcat.shape[1]
    total = xbuf.shape[1]
    piece = total // nz
    last = 2 * (half - 1)

    def at_x(offset, core):
        return (part, lax.rem(x + offset + NX, NX) * nz + z, core)

    def at_z(where, core):
        return (part, x * nz + where, core)

    sibling = (part, dp, 1 - c)
    partner = (mate, dp, c)
    up, down = lax.rem(z + 1, nz), lax.rem(z + nz - 1, nz)

    barrier = pltpu.get_barrier_semaphore()
    greeted = [at_x(o, k) for o in range(1, NX) for k in (0, 1)]
    greeted += [sibling, partner, at_z(up, c), at_z(down, c)]
    for device in greeted:
        pl.semaphore_signal(barrier, inc=1, device_id=device, device_id_type=pl.DeviceIdType.MESH)
    pl.semaphore_wait(barrier, len(greeted))

    def w_block(xs, zs):
        return wbuf.at[pl.ds(pl.multiple_of((xs * nz + zs) * rows, rows), rows), :]

    def w0(b):
        return remote(
            wcat.at[b], w_block(x, z), w0_s.at[b], w0_r.at[lax.rem(x, 2)],
            (part, (2 * c + b) * nz + z, lax.div(x, 2)),
        )

    def w0_here(b):
        return pltpu.make_async_copy(wcat.at[b], w_block(x, z), w0_s.at[b])

    for b in (0, 1):
        pl.when(2 * c + b != x)(lambda b=b: w0(b).start())

    for b in (0, 1):
        @pl.when(2 * c + b == x)
        def _(b=b):
            w_block(x, z)[...] = wcat[b]

    meta[x] = meta_ref[...]

    def meta_copy(o):
        return remote(meta_ref, meta.at[x], meta_s.at[o], meta_r.at[o], at_x(o, c))

    for o in range(1, NX):
        meta_copy(o).start()

    quarter = total // 4
    away = [lax.rem(x - 2 * c - s + 2 * NX, NX) for s in (0, 1)]
    is_source = lax.div(x, 2) == c
    mine = lax.rem(x, 2)

    def x_rows(q):
        return pl.ds(q * quarter, quarter)

    def x_send(direction, q):
        return remote(
            x_hbm.at[x_rows(q)], xbuf.at[mine, x_rows(q)], x_s.at[direction, q], x_r.at[mine, q],
            at_x(1 if direction == 0 else -1, c),
        )

    def x_local():
        return pltpu.make_async_copy(x_hbm, xbuf.at[mine], x_l)

    def x_forward(s, q, direction):
        return remote(
            xbuf.at[s, x_rows(q)], xbuf.at[s, x_rows(q)], xf_s.at[s, q % 2], x_r.at[s, q],
            at_x(1 if direction == 0 else -1, c),
        )

    @pl.when(is_source)
    def _():
        for i in range(4):
            x_send(0, i).start()
            x_send(1, (i + 2) % 4).start()
        x_local().start()

    def pass_on(i):
        for s in (0, 1):
            @pl.when(away[s] == 1)
            def _(s=s):
                x_forward(s, i, 0).wait_recv()
                x_forward(s, i, 0).start()

            @pl.when(away[s] == 3)
            def _(s=s):
                x_forward(s, 2 + i, 1).wait_recv()
                x_forward(s, 2 + i, 1).start()

    def hop(direction, zs, idx):
        blk = w_block(2 * c + yb, zs)
        return remote(blk, blk, ring_s.at[idx], ring_r.at[idx], at_z(up if direction == 0 else down, c))

    def to_sibling(zs, idx):
        blk = w_block(2 * c + yb, zs)
        return remote(blk, blk, sib_s.at[idx], sib_r.at[idx], sibling)

    def from_sibling(zs, idx):
        blk = w_block(2 * (1 - c) + yb, zs)
        return remote(blk, blk, sib_s.at[idx], sib_r.at[idx], sibling)

    def to_partner(zs, idx):
        blk = w_block(2 * c + yb, zs)
        return remote(blk, blk, y_s.at[idx], y_r.at[idx], partner)

    def from_partner(zs, idx):
        blk = w_block(2 * c + 1 - yb, zs)
        return remote(blk, blk, y_s.at[idx], y_r.at[idx], partner)

    def y_to_sibling(zs, idx):
        blk = w_block(2 * c + 1 - yb, zs)
        return remote(blk, blk, ysib_s.at[idx], ysib_r.at[idx], sibling)

    def own_to_sibling(i):
        blk = w_block(2 * c + i, z)
        return remote(blk, blk, own_s.at[i], own_r.at[i], sibling)

    def o_block(zs, core):
        return wobuf.at[core, pl.ds(pl.multiple_of(zs * QC, QC), QC), :]

    def o_hop(direction, zs, idx, src=None):
        blk = o_block(zs, c)
        return remote(
            blk if src is None else src, blk, o_s.at[idx], o_r.at[idx],
            at_z(up if direction == 0 else down, c),
        )

    def o_sibling(zs, idx):
        blk = o_block(zs, c)
        return remote(blk, blk, osib_s.at[idx], osib_r.at[idx], sibling)

    def o_own_sibling():
        return remote(o_t, o_block(z, c), oown_s, oown_r, sibling)

    for i in (0, 1):
        @pl.when(2 * c + i != x)
        def _(i=i):
            remote(wcat.at[0], w_block(2 * c + i, z), w0_s.at[0], w0_r.at[i], sibling).wait_recv()

    first = (0, half - 1)
    for direction in (0, 1):
        hop(direction, z, first[direction]).start()
    for i in (0, 1):
        own_to_sibling(i).start()
    for direction in (0, 1):
        o_hop(direction, z, first[direction], o_t).start()
    o_own_sibling().start()
    o_block(z, c)[...] = o_t[...]

    def block_of(direction, k):
        return lax.rem(z + (nz - k if direction == 0 else k), nz)

    def partner_on(direction, k, idx):
        zs = block_of(direction, k)
        from_partner(zs, idx).wait_recv()
        y_to_sibling(zs, idx).start()

    def ring_step(k, carry):
        for direction in (0, 1):
            idx = direction * (half - 1) + k - 1
            nxt = jnp.where(k == half - 1, last, idx + 1)
            zs = block_of(direction, k)
            hop(direction, zs, idx).wait_recv()

            @pl.when((k < half - 1) | (c == direction))
            def _():
                hop(direction, zs, nxt).start()

            to_sibling(zs, idx).start()
            to_partner(zs, idx).start()
        for direction in (0, 1):
            idx = direction * (half - 1) + k - 1
            nxt = jnp.where(k == half - 1, last, idx + 1)
            zs = block_of(direction, k)
            o_hop(direction, zs, idx).wait_recv()

            @pl.when((k < half - 1) | (c == direction))
            def _():
                o_hop(direction, zs, nxt).start()

            o_sibling(zs, idx).start()

        @pl.when(k > 1)
        def _():
            for direction in (0, 1):
                partner_on(direction, k - 1, direction * (half - 1) + k - 2)

        return carry

    lax.fori_loop(1, 3, ring_step, 0)
    pass_on(0)
    lax.fori_loop(3, 5, ring_step, 0)
    pass_on(1)
    lax.fori_loop(5, half, ring_step, 0)
    far = block_of(0, half)
    hop(0, far, last).wait_recv()
    to_sibling(far, last).start()
    to_partner(far, last).start()
    for direction in (0, 1):
        partner_on(direction, half - 1, direction * (half - 1) + half - 2)
    o_hop(0, far, last).wait_recv()
    o_sibling(far, last).start()
    from_partner(far, last).wait_recv()
    y_to_sibling(far, last).start()

    def arrived(idx, carry):
        from_sibling(z, idx).wait_recv()
        remote(w_block(2 * c, z), w_block(2 * c, z), ysib_s.at[idx], ysib_r.at[idx], sibling).wait_recv()
        remote(o_block(z, c), o_block(z, c), osib_s.at[idx], osib_r.at[idx], sibling).wait_recv()
        return carry

    lax.fori_loop(0, last + 1, arrived, 0)
    for i in (0, 1):
        own_to_sibling(i).wait_recv()
    o_own_sibling().wait_recv()
    for s in (0, 1):
        @pl.when(away[s] == 1)
        def _(s=s):
            for q in (2, 3):
                x_forward(s, q, 0).wait_recv()

        @pl.when(away[s] == 3)
        def _(s=s):
            for q in (0, 1):
                x_forward(s, q, 0).wait_recv()

        @pl.when(away[s] == 2)
        def _(s=s):
            for q in range(4):
                x_forward(s, q, 0).wait_recv()

    @pl.when(is_source)
    def _():
        x_local().wait()

    for o in range(1, NX):
        meta_copy(o).wait_recv()

    lane = lax.broadcasted_iota(jnp.int32, (1, HD), 1)
    row = jnp.zeros((1, HD), jnp.int32)
    for j in range(NX):
        row = jnp.where(lane == j, meta[j, pl.ds(0, 1), :], row)
    dests[z] = row

    cosine, sine = cos_ref[...], sin_ref[...]

    def rotated(u):
        return u * cosine + pltpu.roll(u, HD // 2, 1) * sine

    groups = (acc.shape[1] - 2 * HD) // HD
    key_at = lax.broadcasted_iota(jnp.int32, (total, total), 1)
    query_at = lax.broadcasted_iota(jnp.int32, (total, total), 0)
    position = lax.broadcasted_iota(jnp.int32, (total, HD), 0)

    def a_send(s, direction):
        return remote(
            att.at[s, x], att.at[s, x], a_s.at[s, direction], a_r.at[s, direction],
            at_x(1 if direction == 0 else -1, c),
        )

    def a_forward(s):
        blk = att.at[s, lax.rem(x + (NX - 1 if s == 0 else 1), NX)]
        return remote(blk, blk, af_s.at[s], a_r.at[s, 2], at_x(1 if s == 0 else -1, c))

    for s in (0, 1):
        acc[...] = jnp.zeros_like(acc)

        def project(i, carry, s=s):
            cols = pl.ds(pl.multiple_of(i * KC, KC), KC)
            acc[...] += jnp.dot(xbuf[s, :, cols], wbuf[cols, :], preferred_element_type=jnp.float32)
            return carry

        lax.fori_loop(0, wbuf.shape[0] // KC, project, 0)
        length = meta[2 * c + s, pl.ds(1, 1), :]
        keys = rotated(acc[:, groups * HD : (groups + 1) * HD])
        values = acc[:, (groups + 1) * HD :]
        live = position < length
        kept_keys = jnp.where(live, keys, 0.0).astype(jnp.bfloat16)
        kept_values = jnp.where(live, values, 0.0).astype(jnp.bfloat16)

        @pl.when(c == 0)
        def _(s=s, kept_keys=kept_keys, kept_values=kept_values):
            kvall[s] = kept_keys
            swap[s] = kept_values

        @pl.when(c == 1)
        def _(s=s, kept_keys=kept_keys, kept_values=kept_values):
            kvall[2 + s] = kept_values
            swap[s] = kept_keys

        keys = keys.astype(jnp.bfloat16)
        values = values.astype(jnp.bfloat16)
        wide = jnp.concatenate([length] * (total // HD), axis=1)
        allowed = (query_at >= key_at) & (key_at < wide)
        for g in range(groups):
            query = rotated(acc[:, g * HD : (g + 1) * HD]).astype(jnp.bfloat16)
            scores = lax.dot_general(
                query, keys, (((1,), (1,)), ((), ())), preferred_element_type=jnp.float32
            ) * (1.0 / math.sqrt(HD))
            scores = jnp.where(allowed, scores, -jnp.inf)
            expo = jnp.exp(scores - jnp.max(scores, axis=1, keepdims=True))
            weights = (expo / jnp.sum(expo, axis=1, keepdims=True)).astype(jnp.bfloat16)
            att[s, x, :, g * HD : (g + 1) * HD] = jnp.dot(
                weights, values, preferred_element_type=jnp.float32
            ).astype(jnp.bfloat16)
        for direction in (0, 1):
            a_send(s, direction).start()

    def swapped():
        return remote(swap, kvall.at[pl.ds(2 * c, 2)], swap_s, swap_r, sibling)

    swapped().start()

    def d_copy(o):
        return remote(dests.at[z], dests.at[z], dest_s.at[o], dest_r.at[o], at_z(lax.rem(z + o, nz), c))

    def c1_copy(o):
        to = lax.rem(z + o, nz)
        return remote(
            kvall.at[:, pl.ds(pl.multiple_of(to * piece, piece), piece), :],
            spread.at[pl.ds(z * NX, NX)],
            c1_s.at[o], c1_r.at[o], at_z(to, c),
        )

    def send_dest(o, carry):
        d_copy(o).start()
        return carry

    lax.fori_loop(1, nz, send_dest, 0)
    swapped().wait_recv()

    def send_c1(o, carry):
        c1_copy(o).start()
        return carry

    lax.fori_loop(1, nz, send_c1, 0)
    spread[pl.ds(z * NX, NX)] = kvall[:, pl.ds(pl.multiple_of(z * piece, piece), piece), :]

    def head_rows(s, xs):
        core = lax.div(xs, 2)
        cols = pl.ds(pl.multiple_of(lax.rem(xs, 2) * att.shape[3], att.shape[3]), att.shape[3])
        return lax.dot_general(
            att[s, xs], wobuf[core, :, cols], (((1,), (1,)), ((), ())),
            preferred_element_type=jnp.float32,
        )

    for s in (0, 1):
        oacc[s] = head_rows(s, x)
    for s in (0, 1):
        for direction in (0, 1):
            a_send(s, direction).wait_recv()
            if direction == s:
                a_forward(s).start()
    for s in (0, 1):
        for direction in (0, 1):
            oacc[s] += head_rows(s, lax.rem(x + (NX - 1 if direction == 0 else 1), NX))

    def d_wait(o, carry):
        d_copy(o).wait_recv()
        c1_copy(o).wait_recv()
        return carry

    lax.fori_loop(1, nz, d_wait, 0)
    all_dests = dests[...].reshape(nz, HD)
    lanes = lax.broadcasted_iota(jnp.int32, (nz, HD), 1)
    prompt = lax.broadcasted_iota(jnp.int32, (nz, HD), 0) * NX
    source = jnp.zeros((nz, HD), jnp.int32)
    for j in range(NX):
        slot = jnp.sum(jnp.where(lanes == j, all_dests, 0), axis=1, keepdims=True)
        source += jnp.where(slot == lanes, prompt + j, 0)
    srcv[...] = jnp.minimum(jnp.sum(source, axis=0, keepdims=True), NX * nz - 1)
    to_scalars = pltpu.make_async_copy(srcv, srcs, src_l)
    to_scalars.start()
    to_scalars.wait()

    def reorder(d, carry):
        perm[d] = spread[srcs[0, d]]
        return carry

    lax.fori_loop(0, NX * nz, reorder, 0)

    def c2_copy(o):
        to = lax.rem(x + o, NX)
        return remote(
            perm.at[pl.ds(to * nz, nz)], heads.at[x], c2_s.at[o], c2_r.at[o], at_x(o, c)
        )

    for o in range(1, NX):
        c2_copy(o).start()
    heads[x] = perm[pl.ds(x * nz, nz)]

    width = oacc.shape[2]

    def out_copy(s):
        to = 2 * c + s
        cols = pl.ds(pl.multiple_of(lax.rem(x, 2) * width, width), width)
        return remote(
            obuf.at[s], out_hbm.at[:, cols], out_s.at[s], out_r.at[lax.rem(x, 2)],
            (part, to * nz + z, lax.div(x, 2)),
        )

    def out_here(s):
        cols = pl.ds(pl.multiple_of(lax.rem(x, 2) * width, width), width)
        return pltpu.make_async_copy(obuf.at[s], out_hbm.at[:, cols], out_l)

    for s in (0, 1):
        a_forward(s).wait_recv()
        obuf[s] = (oacc[s] + head_rows(s, lax.rem(x + 2, NX))).astype(jnp.bfloat16)
        pl.when(2 * c + s != x)(lambda s=s: out_copy(s).start())
        pl.when(2 * c + s == x)(lambda s=s: out_here(s).start())

    for o in range(1, NX):
        c2_copy(o).wait_recv()
    target = lax.div(z, half)
    place = pl.ds(pl.multiple_of(lax.rem(z, half) * piece, piece), piece)

    def c3_copy(o):
        to = lax.rem(z + o, nz)
        return remote(
            heads.at[:, to], kv_hbm.at[c, :, place, :], c3_s.at[o], c3_r.at[c, lax.rem(z, half)],
            at_z(to, target),
        )

    def c3_here():
        return pltpu.make_async_copy(heads.at[:, z], kv_hbm.at[c, :, place, :], c3_l)

    def send_c3(o, carry):
        c3_copy(o).start()
        return carry

    lax.fori_loop(1, nz, send_c3, 0)
    pl.when(target == c)(lambda: c3_here().start())
    pl.when(target != c)(lambda: c3_copy(0).start())

    def c3_wait(i, carry):
        kind, zs = lax.div(i, half), lax.rem(i, half)

        @pl.when((kind != c) | (half * c + zs != z))
        def _():
            remote(
                heads.at[:, z],
                kv_hbm.at[kind, :, pl.ds(pl.multiple_of(zs * piece, piece), piece), :],
                c3_s.at[0], c3_r.at[kind, zs], sibling,
            ).wait_recv()

        return carry

    lax.fori_loop(0, nz, c3_wait, 0)
    pl.when(target == c)(lambda: c3_here().wait())
    pl.when(target != c)(lambda: c3_copy(0).wait_send())
    for i in (0, 1):
        @pl.when(2 * c + i != x)
        def _(i=i):
            cols = pl.ds(i * width, width)
            remote(obuf.at[0], out_hbm.at[:, cols], out_s.at[0], out_r.at[i], sibling).wait_recv()

    for s in (0, 1):
        pl.when(2 * c + s != x)(lambda s=s: out_copy(s).wait_send())
        pl.when(2 * c + s == x)(lambda s=s: out_here(s).wait())
        for direction in (0, 1):
            a_send(s, direction).wait_send()
        a_forward(s).wait_send()
    for b in (0, 1):
        pl.when(2 * c + b != x)(lambda b=b: w0(b).wait_send())
    for o in range(1, NX):
        meta_copy(o).wait_send()
        c2_copy(o).wait_send()

    @pl.when(is_source)
    def _():
        for i in range(4):
            for direction in (0, 1):
                x_send(direction, i).wait_send()

    for s in (0, 1):
        for i in (0, 1):
            pl.when(away[s] == 1)(lambda s=s, i=i: x_forward(s, i, 0).wait_send())
            pl.when(away[s] == 3)(lambda s=s, i=i: x_forward(s, 2 + i, 1).wait_send())
        own_to_sibling(s).wait_send()
    o_own_sibling().wait_send()
    swapped().wait_send()

    def drain_z(o, carry):
        d_copy(o).wait_send()
        c1_copy(o).wait_send()
        c3_copy(o).wait_send()
        return carry

    lax.fori_loop(1, nz, drain_z, 0)

    def drain_ring(idx, carry):
        hop(0, z, idx).wait_send()
        to_sibling(z, idx).wait_send()
        to_partner(z, idx).wait_send()
        y_to_sibling(z, idx).wait_send()
        o_hop(0, z, idx).wait_send()
        o_sibling(z, idx).wait_send()
        return carry

    lax.fori_loop(0, last + 1, drain_ring, 0)


def on_device(normed, q_weight, kv_weight, o_weight, lengths, destinations):
    tokens = normed[0]
    total, width = tokens.shape
    nz = lax.axis_size("dp") // NX
    rows = q_weight.shape[0]
    q_cols = q_weight.shape[1] // 2
    q_parts = q_weight.reshape(rows, 2, q_cols).transpose(1, 0, 2)
    kv_parts = kv_weight.reshape(rows, 2, 2, HD).transpose(2, 0, 1, 3).reshape(2, rows, 2 * HD)
    wcat = jnp.concatenate([q_parts, kv_parts], axis=-1)
    o_t = o_weight.T
    cosine, sine = tables(total)
    meta = jnp.stack(
        [jnp.broadcast_to(destinations, (HD,)), jnp.broadcast_to(lengths, (HD,))]
    )
    columns = q_cols + 2 * HD
    o_cols = rows * nz
    piece = total // nz
    hops = nz - 1
    bf16, f32 = jnp.bfloat16, jnp.float32
    dma = pltpu.SemaphoreType.DMA
    scratch = [
        pltpu.VMEM((width, columns), bf16),
        pltpu.VMEM((2, o_cols, o_weight.shape[0]), bf16),
        pltpu.VMEM((2, total, width), bf16),
        pltpu.VMEM((2, NX, total, q_cols), bf16),
        pltpu.VMEM((total, columns), f32),
        pltpu.VMEM((2, total, o_cols), f32),
        pltpu.VMEM((2, total, o_cols), bf16),
        pltpu.VMEM((NX, 2, HD), jnp.int32),
        pltpu.VMEM((nz, 1, HD), jnp.int32),
        pltpu.VMEM((1, HD), jnp.int32),
        pltpu.SMEM((1, HD), jnp.int32),
        pltpu.VMEM((NX, total, HD), bf16),
        pltpu.VMEM((2, total, HD), bf16),
        pltpu.VMEM((NX * nz, piece, HD), bf16),
        pltpu.VMEM((NX * nz, piece, HD), bf16),
        pltpu.VMEM((NX, nz, piece, HD), bf16),
    ]
    shapes = [
        (NX,), (NX,), (2,), (2,), (hops,), (hops,), (hops,), (hops,), (hops,), (hops,), (hops,), (hops,), (2,), (2,),
        (hops,), (hops,), (hops,), (hops,), None, None, None, (2, 4), (2, 2), (2, 4), (2, 2), (2,), (2, 3), None, None,
        (nz,), (nz,), (nz,), (nz,), None, (NX,), (NX,), (nz,), (2, nz // 2), None, (2,), (2,), None,
    ]
    scratch += [dma if shape is None else dma(shape) for shape in shapes]
    vmem = pl.BlockSpec(memory_space=pltpu.VMEM)
    any_space = pl.BlockSpec(memory_space=pl.ANY)
    projected, cache = pl.pallas_call(
        functools.partial(kernel, nz),
        out_shape=(
            jax.ShapeDtypeStruct((total, 2 * o_cols), bf16),
            jax.ShapeDtypeStruct((2, NX, total // 2, HD), bf16),
        ),
        in_specs=[any_space, vmem, vmem, vmem, vmem, vmem],
        out_specs=(any_space, any_space),
        scratch_shapes=scratch,
        compiler_params=pltpu.CompilerParams(
            collective_id=0, has_side_effects=True, vmem_limit_bytes=60 * 1024 * 1024
        ),
    )(tokens, wcat, o_t, cosine, sine, meta)
    return (projected[None], cache[None])


def solution(mesh):
    placed = (
        P(("parts", "dp"), None, None),
        P("dp", "tensor"),
        P("dp", None, "tensor"),
        P("tensor", "dp"),
        P(("parts", "dp")),
        P(("parts", "dp")),
    )
    return jax.shard_map(
        on_device,
        mesh=mesh,
        in_specs=placed,
        out_specs=(
            P(("parts", "dp"), None, "tensor"),
            P(("parts", "dp"), None, None, "tensor", None),
        ),
        check_vma=False,
    )
```

time: 403 us -> 133 us (0.33)
  waiting for transfers between devices: 268 us -> 0 us
  Pallas kernels: 0 us -> 121 us
  starting transfers between devices: 65.3 us -> 0 us
  matrix products: 22.4 us -> 0 us
  between operations: 15.6 us -> 2.01 us
  other arithmetic: 13.7 us -> 2.04 us
  blocking collectives: 6.76 us -> 0 us
  local copies, waits for them, and re-layouts: 9.6 us -> 4.71 us
    all_gather x2 -> x0, waiting for transfers between devices: 243 us -> none  [the longest x1 135 us: in_one_piece(): filled = lax.all_gather(both, axis, axis=dim, tiled=True)]
    pallas_call x0 -> x1, Pallas kernels: none -> 121 us  [on_device(): pl.pallas_call(functools.partial(kernel, nz), out_shape=(jax.ShapeDtypeSt...]
    all_to_all x4 -> x0, starting transfers between devices: 65.2 us -> none  [the longest x1 29.6 us: copy_for_each(): return lax.all_to_all(copies, axis, split_axis=0, concat_axis=0, tiled=True)]
    all_to_all x4 -> x0, waiting for transfers between devices: 24.4 us -> none  [the longest x1 14.4 us: deliver(): lax.all_to_all(outgoing, 'dp', split_axis=0, concat_axis=0, tiled=True)]
    dot_general x4 -> x0, matrix products: 18.9 us -> none  [the longest x1 7.7 us: on_device(): jnp.dot(attended, lax.all_gather(o_weight, 'dp', axis=1, tiled=True), pre...]
    all_to_all x1 -> x0, blocking collectives: 6.76 us -> none  [regroup(): lax.all_to_all(cache, 'tensor', split_axis=2, concat_axis=1, tiled=True)]
    all_to_all x3 -> x0, other arithmetic: 4.85 us -> none  [the longest x1 2.12 us: deliver(): spread = lax.all_to_all(flat, 'dp', split_axis=0, concat_axis=0, tiled=True)]
  transfers between devices with their start and end apart: 6 -> 0, of which waited for: 5 -> 0; matrix products, arithmetic and copies ran while one was open for 10% -> 0% of each run, Pallas kernels for 0% -> 0%
where the time goes in v1:
time: 133 us; the launch traced here: 130 us
  Pallas kernels  121 us (91%)
  local copies, waits for them, and re-layouts  4.71 us (4%)
  other arithmetic  2.04 us (2%)
  between operations  2.01 us (2%)
    pallas_call x1, Pallas kernels, on_device(): pl.pallas_call(functools.partial(kernel, nz), out_shape=(jax.ShapeDtypeSt...  121 us
    unnamed x6, local copies, waits for them, and re-layouts  3.06 us

profile of v1, /device:TPU:33, one launch (start us, length us, event | category | flops | bytes accessed | tf_op | source)
XLA Modules:
  0.0 130.1 jit_solution(4257058214102801324)
XLA Ops:
  0.6 0.0 copy-start
  2.0 0.6 stack.6.meta_ref
  2.6 0.0 copy-done
  2.7 0.9 copy.15
  3.7 0.7 pad_maximum_fusion.wcat
  4.3 0.5 fusion.2
  4.9 0.8 pad_maximum_fusion.1
  5.7 121.4 %shard_map.80 = (bf16[256,2048]{1,0:T(8,128)(2,1)}, bf16[2,4,128,128]{3,2,1,0:T(8,128)(2,1)}) custom-call(bf16[256,4096]{1,0:T(8,128)(2,1)} %bitcast.20, bf16[2,64,768]{2,1,0:T(8,128)(2,1)} %pad_maximum_fusion.wcat, bf16[64,1024]{1,0:T(8,128)(2,1)} %bitcast.24, f32[256,128]{1,0:T(8,128)} %get-tuple-element.9.cos_ref, f32[256,128]{1,0:T(8,128)} %get-tuple-element.10.sin_ref, ...), custom_call_target="tpu_custom_call" | custom-call | tf_op jit(solution)/shard_map/pallas_call | solution.py:604
  127.1 0.0 copy-start.1
  127.1 2.3 %copy.20 = bf16[1,256,2048]{2,1,0:T(8,128)(2,1)} copy(bf16[1,256,2048]{2,1,0:T(8,128)(2,1)} %bitcast.21) | data formatting | bytes 2097152
  129.4 0.0 copy-done.1
  129.4 0.7 copy.21
  (4 shorter events, 0.1 us)
Async XLA Ops:
  0.6 2.0 %copy-start = (bf16[64,2,256]{2,1,0:T(2,128)(2,1)S(1)}, bf16[64,2,256]{2,1,0:T(2,128)(2,1)}, u32[]{:S(2)}) copy-start(bf16[64,2,256]{2,1,0:T(2,128)(2,1)} %param.8) | copy-start | bytes 196612
  127.1 2.4 %copy-start.1 = (bf16[2,4,128,128]{3,2,1,0:T(8,128)(2,1)S(1)}, bf16[2,4,128,128]{3,2,1,0:T(8,128)(2,1)}, u32[]{:S(2)}) copy-start(bf16[2,4,128,128]{3,2,1,0:T(8,128)(2,1)} %get-tuple-element.5) | copy-start | bytes 786436

commit v2 on v1

v2 whole, which is shorter than its diff:
```python
import functools
import math

import jax
import jax.numpy as jnp
import numpy as np
from jax import lax
from jax.experimental import pallas as pl
from jax.experimental.pallas import tpu as pltpu
from jax.sharding import PartitionSpec as P

HD = 128
ROPE_BASE = 500000.0
NX = 4
KC = 512
QC = 64
LAG = 1


def tables(total):
    half = HD // 2
    steps = np.arange(half, dtype=np.float32) * np.float32(2.0 / HD)
    freq = np.power(np.float32(ROPE_BASE), -steps)
    angle = np.arange(total, dtype=np.float32)[:, None] * freq[None, :]
    cosine, sine = np.cos(angle), np.sin(angle)
    return (
        jnp.asarray(np.concatenate([cosine, cosine], axis=-1)),
        jnp.asarray(np.concatenate([-sine, sine], axis=-1)),
    )


def remote(src, dst, send, recv, device):
    return pltpu.make_async_remote_copy(
        src_ref=src,
        dst_ref=dst,
        send_sem=send,
        recv_sem=recv,
        device_id=device,
        device_id_type=pl.DeviceIdType.MESH,
    )


def kernel(
    nz, x_hbm, q_ref, kv_ref, o_t, cos_ref, sin_ref, dest_ref, length_ref, out_hbm, kv_hbm,
    wbuf, wobuf, xbuf, att, acc, oacc, obuf, meta, dests, srcv, srcs, kvall, swap, spread, perm, heads,
    meta_s, meta_r, w0_s, w0_r, ring_s, ring_r, sib_s, sib_r, y_s, y_r, ysib_s, ysib_r, own_s, own_r,
    o_s, o_r, osib_s, osib_r, oown_s, oown_r, x_l, x_s, xf_s, x_r, a_s, af_s, a_r, swap_s, swap_r,
    dest_s, dest_r, c1_s, c1_r, src_l, c2_s, c2_r, c3_s, c3_r, c3_l, out_s, out_r, out_l, ready, kvbuf, relay, relay_s, relay_r,
    oy_s, oy_r, oysib_s, oysib_r,
):
    part, dp, c = lax.axis_index("parts"), lax.axis_index("dp"), lax.axis_index("tensor")
    x, z = lax.div(dp, nz), lax.rem(dp, nz)
    half = nz // 2
    yb = lax.rem(part, 2)
    mate = part + 1 - 2 * yb
    rows = q_ref.shape[0]
    total = xbuf.shape[1]
    piece = total // nz
    last = 2 * (half - 1)

    def at_x(offset, core):
        return (part, lax.rem(x + offset + NX, NX) * nz + z, core)

    def at_z(where, core):
        return (part, x * nz + where, core)

    sibling = (part, dp, 1 - c)
    partner = (mate, dp, c)
    up, down = lax.rem(z + 1, nz), lax.rem(z + nz - 1, nz)

    barrier = pltpu.get_barrier_semaphore()

    def greet(semaphore, device):
        pl.semaphore_signal(semaphore, inc=1, device_id=device, device_id_type=pl.DeviceIdType.MESH)

    greeted = [at_x(o, k) for o in range(1, NX) for k in (0, 1)] + [sibling, partner]
    for device in greeted:
        greet(barrier, device)
    pl.when(z != 0)(lambda: greet(barrier, at_z(up, c)))
    pl.when(z == 1)(lambda: greet(barrier, at_z(down, c)))
    pl.semaphore_wait(
        barrier, len(greeted) + jnp.where(z == 1, 0, 1) + jnp.where(z == 0, 1, 0)
    )
    pl.when(z != 1)(lambda: greet(ready.at[0], at_z(down, c)))
    pl.when(z == 0)(lambda: greet(ready.at[1], at_z(up, c)))

    columns = wbuf.shape[1]
    q_cols = columns - 2 * HD

    def w_block(xs, zs):
        return wbuf.at[pl.ds(pl.multiple_of((xs * nz + zs) * rows, rows), rows), :]

    def w0_parts(b):
        return (
            (q_ref, b * q_cols, 0, q_cols),
            (kv_ref, b * HD, q_cols, HD),
            (kv_ref, (2 + b) * HD, q_cols + HD, HD),
        )

    def w0(b):
        block = w_block(x, z)
        return [
            remote(
                src.at[:, pl.ds(start, size)], block.at[:, pl.ds(to, size)], w0_s.at[b, i],
                w0_r.at[lax.rem(x, 2)], (part, (2 * c + b) * nz + z, lax.div(x, 2)),
            )
            for i, (src, start, to, size) in enumerate(w0_parts(b))
        ]

    for b in (0, 1):
        @pl.when(2 * c + b != x)
        def _(b=b):
            for copy in w0(b):
                copy.start()

    for b in (0, 1):
        @pl.when(2 * c + b == x)
        def _(b=b):
            block = w_block(x, z)
            for src, start, to, size in w0_parts(b):
                block[:, to : to + size] = src[:, start : start + size]

    meta[x] = jnp.concatenate(
        [jnp.full((1, HD), dest_ref[0], jnp.int32), jnp.full((1, HD), length_ref[0], jnp.int32)]
    )

    def meta_copy(o):
        return remote(meta.at[x], meta.at[x], meta_s.at[o], meta_r.at[o], at_x(o, c))

    for o in range(1, NX):
        meta_copy(o).start()

    quarter = total // 4

    def away(s):
        return lax.rem(x - 2 * c - s + 2 * NX, NX)

    is_source = lax.div(x, 2) == c
    mine = lax.rem(x, 2)

    def x_rows(q):
        return pl.ds(q * quarter, quarter)

    def x_send(direction, q):
        return remote(
            x_hbm.at[x_rows(q)], xbuf.at[mine, x_rows(q)], x_s.at[direction, q], x_r.at[mine, q],
            at_x(1 if direction == 0 else -1, c),
        )

    def x_local():
        return pltpu.make_async_copy(x_hbm, xbuf.at[mine], x_l)

    def x_forward(s, q, direction):
        return remote(
            xbuf.at[s, x_rows(q)], xbuf.at[s, x_rows(q)], xf_s.at[s, q % 2], x_r.at[s, q],
            at_x(1 if direction == 0 else -1, c),
        )

    @pl.when(is_source)
    def _():
        for i in range(4):
            x_send(0, i).start()
            x_send(1, (i + 2) % 4).start()
        x_local().start()

    def x_arrival(s, q):
        rows_of = xbuf.at[s, x_rows(q)]
        return remote(rows_of, rows_of, xf_s.at[s, q % 2], x_r.at[s, q], sibling)

    def pass_on(i):
        for s in (0, 1):
            @pl.when(away(s) == 1)
            def _(s=s):
                x_forward(s, i, 0).wait_recv()
                x_forward(s, i, 0).start()

            @pl.when(away(s) == 3)
            def _(s=s):
                x_forward(s, 2 + i, 1).wait_recv()
                x_forward(s, 2 + i, 1).start()

    def hop(direction, zs, idx, part_of):
        first_row = ((2 * c + yb) * nz + zs) * rows + part_of * (rows // 2)
        blk = wbuf.at[pl.ds(pl.multiple_of(first_row, rows // 2), rows // 2), :]
        return remote(
            blk, blk, ring_s.at[idx, part_of], ring_r.at[idx, part_of],
            at_z(up if direction == 0 else down, c),
        )

    def to_sibling(zs, idx):
        blk = w_block(2 * c + yb, zs)
        return remote(blk, blk, sib_s.at[idx], sib_r.at[idx], sibling)

    def from_sibling(zs, idx):
        blk = w_block(2 * (1 - c) + yb, zs)
        return remote(blk, blk, sib_s.at[idx], sib_r.at[idx], sibling)

    def to_partner(zs, idx):
        blk = w_block(2 * c + yb, zs)
        return remote(blk, blk, y_s.at[idx], y_r.at[idx], partner)

    def from_partner(zs, idx):
        blk = w_block(2 * c + 1 - yb, zs)
        return remote(blk, blk, y_s.at[idx], y_r.at[idx], partner)

    def y_to_sibling(zs, idx):
        blk = w_block(2 * c + 1 - yb, zs)
        return remote(blk, blk, ysib_s.at[idx], ysib_r.at[idx], sibling)

    def own_to_sibling(i):
        blk = w_block(2 * c + i, z)
        return remote(blk, blk, own_s.at[i], own_r.at[i], sibling)

    def o_block(zs, core):
        return wobuf.at[core, pl.ds(pl.multiple_of(zs * QC, QC), QC), :]

    def o_part(zs, which):
        start = pl.multiple_of(zs * QC + which * (QC // 2), QC // 2)
        return wobuf.at[c, pl.ds(start, QC // 2), :]

    def o_hop(direction, zs, idx, src=None):
        blk = o_part(zs, yb)
        return remote(
            blk if src is None else src, blk, o_s.at[idx], o_r.at[idx],
            at_z(up if direction == 0 else down, c),
        )

    def o_sibling(zs, idx):
        blk = o_part(zs, yb)
        return remote(blk, blk, osib_s.at[idx], osib_r.at[idx], sibling)

    def o_partner(zs, idx):
        blk = o_part(zs, yb)
        return remote(blk, blk, oy_s.at[idx], oy_r.at[idx], partner)

    def o_y_sibling(zs, idx):
        blk = o_part(zs, 1 - yb)
        return remote(blk, blk, oysib_s.at[idx], oysib_r.at[idx], sibling)

    def o_own_sibling():
        return remote(o_t, o_block(z, c), oown_s, oown_r, sibling)

    for i in (0, 1):
        @pl.when(2 * c + i != x)
        def _(i=i):
            blk = w_block(2 * c + i, z)
            remote(blk, blk, w0_s.at[0, 0], w0_r.at[i], sibling).wait_recv()

    first = (0, half - 1)
    for i in (0, 1):
        own_to_sibling(i).start()
    pl.when(z != 0)(lambda: pl.semaphore_wait(ready.at[0], 1))
    for h in (0, 1):
        hop(0, z, first[0], h).start()
    pl.when(z == 1)(lambda: pl.semaphore_wait(ready.at[1], 1))
    for h in (0, 1):
        hop(1, z, first[1], h).start()
    o_block(z, c)[...] = o_t[...]

    def block_of(direction, k):
        return lax.rem(z + (nz - k if direction == 0 else k), nz)

    def slot_of(direction, k):
        return direction * (half - 1) + k - 1

    def partner_on(direction, k, idx):
        zs = block_of(direction, k)
        from_partner(zs, idx).wait_recv()
        y_to_sibling(zs, idx).start()

    def w_half(direction, k, h):
        idx = slot_of(direction, k)
        zs = block_of(direction, k)
        hop(direction, zs, idx, h).wait_recv()

        @pl.when((k < half - 1) | (c == direction))
        def _():
            hop(direction, zs, jnp.where(k == half - 1, last, idx + 1), h).start()

    def w_rest(direction, k):
        idx = slot_of(direction, k)
        zs = block_of(direction, k)
        to_sibling(zs, idx).start()
        to_partner(zs, idx).start()

    def o_step(k):
        for direction in (0, 1):
            idx = slot_of(direction, k)
            zs = block_of(direction, k)
            o_hop(direction, zs, idx).wait_recv()

            @pl.when((k < half - 1) | (c == direction))
            def _(direction=direction, idx=idx, zs=zs):
                o_hop(direction, zs, jnp.where(k == half - 1, last, idx + 1)).start()

            o_sibling(zs, idx).start()

    def ring_step(k, carry):
        for h in (0, 1):
            for direction in (0, 1):
                w_half(direction, k, h)
        for direction in (0, 1):
            w_rest(direction, k)
        @pl.when(k > LAG)
        def _():
            o_step(k - LAG)

        @pl.when(k > 1)
        def _():
            for direction in (0, 1):
                partner_on(direction, k - 1, slot_of(direction, k - 1))

        return carry

    for direction in (0, 1):
        o_hop(direction, z, first[direction], o_t.at[pl.ds(pl.multiple_of(yb * (QC // 2), QC // 2), QC // 2)]).start()
    o_own_sibling().start()
    lax.fori_loop(1, 3, ring_step, 0)
    pass_on(0)
    lax.fori_loop(3, 5, ring_step, 0)
    pass_on(1)
    lax.fori_loop(5, half, ring_step, 0)
    far = block_of(0, half)
    for h in (0, 1):
        hop(0, far, last, h).wait_recv()
    to_sibling(far, last).start()
    to_partner(far, last).start()
    for direction in (0, 1):
        partner_on(direction, half - 1, slot_of(direction, half - 1))
    for k in range(half - LAG, half):
        o_step(k)
    for direction in (0, 1):
        def o_over(k, carry, direction=direction):
            o_partner(block_of(direction, k), slot_of(direction, k)).start()
            return carry

        lax.fori_loop(1, half, o_over, 0)
    from_partner(far, last).wait_recv()
    y_to_sibling(far, last).start()

    def arrived(idx, carry):
        from_sibling(z, idx).wait_recv()
        remote(w_block(2 * c, z), w_block(2 * c, z), ysib_s.at[idx], ysib_r.at[idx], sibling).wait_recv()
        return carry

    lax.fori_loop(0, last + 1, arrived, 0)
    for i in (0, 1):
        own_to_sibling(i).wait_recv()
    for o in range(1, NX):
        meta_copy(o).wait_recv()

    lane = lax.broadcasted_iota(jnp.int32, (1, HD), 1)
    row = jnp.zeros((1, HD), jnp.int32)
    for j in range(NX):
        row = jnp.where(lane == j, meta[j, pl.ds(0, 1), :], row)
    dests[z] = row

    cosine, sine = cos_ref[...], sin_ref[...]

    def rotated(u):
        return u * cosine + pltpu.roll(u, HD // 2, 1) * sine

    groups = q_cols // HD
    key_at = lax.broadcasted_iota(jnp.int32, (total, total), 1)
    query_at = lax.broadcasted_iota(jnp.int32, (total, total), 0)
    position = lax.broadcasted_iota(jnp.int32, (total, HD), 0)

    def a_send(s, direction):
        return remote(
            att.at[s, x], att.at[s, x], a_s.at[s, direction], a_r.at[s, direction],
            at_x(1 if direction == 0 else -1, c),
        )

    def a_forward(s):
        blk = att.at[s, lax.rem(x + (NX - 1 if s == 0 else 1), NX)]
        return remote(blk, blk, af_s.at[s], a_r.at[s, 2], at_x(1 if s == 0 else -1, c))

    def x_wait(s):
        @pl.when(away(s) == 0)
        def _():
            x_local().wait()

        @pl.when((away(s) == 1) | (away(s) == 2))
        def _():
            for q in (2, 3):
                x_arrival(s, q).wait_recv()

        @pl.when((away(s) == 3) | (away(s) == 2))
        def _():
            for q in (0, 1):
                x_arrival(s, q).wait_recv()

    def project(s, start, size):
        cols = pl.ds(start, size)
        acc[s, :, cols] = jnp.zeros((total, size), jnp.float32)

        def part_of(i, carry):
            deep = pl.ds(pl.multiple_of(i * KC, KC), KC)
            acc[s, :, cols] += jnp.dot(
                xbuf[s, :, deep], wbuf[deep, cols], preferred_element_type=jnp.float32
            )
            return carry

        lax.fori_loop(0, wbuf.shape[0] // KC, part_of, 0)

    def cache_rows(s):
        length = meta[2 * c + s, pl.ds(1, 1), :]
        keys = rotated(acc[s, :, q_cols : q_cols + HD])
        values = acc[s, :, q_cols + HD :]
        live = position < length
        kept_keys = jnp.where(live, keys, 0.0).astype(jnp.bfloat16)
        kept_values = jnp.where(live, values, 0.0).astype(jnp.bfloat16)

        @pl.when(c == 0)
        def _():
            kvall[s] = kept_keys
            swap[s] = kept_values

        @pl.when(c == 1)
        def _():
            kvall[2 + s] = kept_values
            swap[s] = kept_keys

        kvbuf[s, 0] = keys.astype(jnp.bfloat16)
        kvbuf[s, 1] = values.astype(jnp.bfloat16)

    def attend(s):
        keys, values = kvbuf[s, 0], kvbuf[s, 1]
        length = meta[2 * c + s, pl.ds(1, 1), :]
        wide = jnp.concatenate([length] * (total // HD), axis=1)
        allowed = (query_at >= key_at) & (key_at < wide)
        for g in range(groups):
            query = rotated(acc[s, :, g * HD : (g + 1) * HD]).astype(jnp.bfloat16)
            scores = lax.dot_general(
                query, keys, (((1,), (1,)), ((), ())), preferred_element_type=jnp.float32
            ) * (1.0 / math.sqrt(HD))
            scores = jnp.where(allowed, scores, -jnp.inf)
            expo = jnp.exp(scores - jnp.max(scores, axis=1, keepdims=True))
            weights = (expo / jnp.sum(expo, axis=1, keepdims=True)).astype(jnp.bfloat16)
            att[s, x, :, g * HD : (g + 1) * HD] = jnp.dot(
                weights, values, preferred_element_type=jnp.float32
            ).astype(jnp.bfloat16)
        for direction in (0, 1):
            a_send(s, direction).start()

    def swapped(s):
        return remote(swap.at[s], kvall.at[2 * c + s], swap_s.at[s], swap_r.at[s], sibling)

    def d_copy(o):
        return remote(dests.at[z], dests.at[z], dest_s.at[o], dest_r.at[o], at_z(lax.rem(z + o, nz), c))

    def c1_copy(o):
        to = lax.rem(z + o, nz)
        return remote(
            kvall.at[:, pl.ds(pl.multiple_of(to * piece, piece), piece), :],
            spread.at[pl.ds(z * NX, NX)],
            c1_s.at[o], c1_r.at[o], at_z(to, c),
        )

    def send_dest(o, carry):
        d_copy(o).start()
        return carry

    def send_c1(o, carry):
        c1_copy(o).start()
        return carry

    apart = away(0)
    near = jnp.where((apart == 1) | (apart == 2), 1, 0)
    lax.fori_loop(1, nz, send_dest, 0)
    for s in (near, 1 - near):
        x_wait(s)
        project(s, q_cols, 2 * HD)
        cache_rows(s)
        swapped(s).start()
    o_hop(0, far, last).wait_recv()
    o_sibling(far, last).start()
    o_partner(far, last).start()
    for s in (0, 1):
        swapped(s).wait_recv()
    lax.fori_loop(1, nz, send_c1, 0)
    spread[pl.ds(z * NX, NX)] = kvall[:, pl.ds(pl.multiple_of(z * piece, piece), piece), :]
    project(near, 0, q_cols)
    attend(near)
    project(1 - near, 0, q_cols)
    attend(1 - near)
    for s in (0, 1):
        a_send(s, s).wait_recv()
        a_forward(s).start()
    def d_wait(o, carry):
        d_copy(o).wait_recv()
        c1_copy(o).wait_recv()
        return carry

    lax.fori_loop(1, nz, d_wait, 0)
    all_dests = dests[...].reshape(nz, HD)
    lanes = lax.broadcasted_iota(jnp.int32, (nz, HD), 1)
    prompt = lax.broadcasted_iota(jnp.int32, (nz, HD), 0) * NX
    source = jnp.zeros((nz, HD), jnp.int32)
    for j in range(NX):
        slot = jnp.sum(jnp.where(lanes == j, all_dests, 0), axis=1, keepdims=True)
        source += jnp.where(slot == lanes, prompt + j, 0)
    srcv[...] = jnp.minimum(jnp.sum(source, axis=0, keepdims=True), NX * nz - 1)
    to_scalars = pltpu.make_async_copy(srcv, srcs, src_l)
    to_scalars.start()
    to_scalars.wait()

    def reorder(d, carry):
        perm[lax.div(d, nz), lax.rem(d, nz)] = spread[srcs[0, d]]
        return carry

    lax.fori_loop(0, NX * nz, reorder, 0)

    def c2_copy(o):
        to = lax.rem(z + o, nz)
        return remote(perm.at[:, to], heads.at[:, z], c2_s.at[o], c2_r.at[o], at_z(to, c))

    def send_c2(o, carry):
        c2_copy(o).start()
        return carry

    lax.fori_loop(1, nz, send_c2, 0)
    heads[:, z] = perm[:, z]

    def o_crossed(idx, carry):
        zs = jnp.where(
            idx == last, far,
            jnp.where(idx < half - 1, block_of(0, idx + 1), block_of(1, idx + 2 - half)),
        )
        o_part_y = o_part(zs, 1 - yb)
        remote(o_part_y, o_part_y, oy_s.at[idx], oy_r.at[idx], partner).wait_recv()
        o_y_sibling(zs, idx).start()
        return carry

    lax.fori_loop(0, last + 1, o_crossed, 0)

    def o_arrived(idx, carry):
        o_sibling(z, idx).wait_recv()
        o_y_sibling(z, idx).wait_recv()
        return carry

    lax.fori_loop(0, last + 1, o_arrived, 0)
    o_own_sibling().wait_recv()

    def head_rows(s, xs):
        core = lax.div(xs, 2)
        cols = pl.ds(pl.multiple_of(lax.rem(xs, 2) * q_cols, q_cols), q_cols)
        return lax.dot_general(
            att[s, xs], wobuf[core, :, cols], (((1,), (1,)), ((), ())),
            preferred_element_type=jnp.float32,
        )

    for s in (0, 1):
        oacc[s] = head_rows(s, x)
    for s in (0, 1):
        a_send(s, 1 - s).wait_recv()
    for s in (0, 1):
        for direction in (0, 1):
            oacc[s] += head_rows(s, lax.rem(x + (NX - 1 if direction == 0 else 1), NX))

    width = oacc.shape[2]

    def out_cols(xs):
        return pl.ds(pl.multiple_of(lax.rem(xs, 2) * width, width), width)

    def out_copy(s):
        return remote(
            obuf.at[s], out_hbm.at[:, out_cols(x)], out_s.at[s, 0], out_r.at[lax.rem(x, 2)],
            (part, (2 * c + s) * nz + z, lax.div(x, 2)),
        )

    def out_here(s):
        return pltpu.make_async_copy(obuf.at[s], out_hbm.at[:, out_cols(x)], out_l)

    def out_rows(direction):
        return pl.ds(direction * (total // 2), total // 2)

    def out_first(s, direction):
        return remote(
            obuf.at[s, out_rows(direction)], relay.at[direction], out_s.at[s, direction],
            relay_r.at[direction], at_x(1 if direction == 0 else -1, c),
        )

    def out_second(direction):
        source = lax.rem(x + (NX - 1 if direction == 0 else 1), NX)
        return remote(
            relay.at[direction], out_hbm.at[out_rows(direction), out_cols(source)],
            relay_s.at[direction], out_r.at[lax.rem(source, 2)],
            at_x(1 if direction == 0 else -1, lax.div(source, 2)),
        )

    def relays(direction):
        to = lax.rem(x + (1 if direction == 0 else NX - 1), NX)
        return lax.div(to, 2) == c

    for s in (0, 1):
        a_forward(s).wait_recv()
        obuf[s] = (oacc[s] + head_rows(s, lax.rem(x + 2, NX))).astype(jnp.bfloat16)

        @pl.when(away(s) == 2)
        def _(s=s):
            for direction in (0, 1):
                out_first(s, direction).start()

        pl.when((away(s) == 1) | (away(s) == 3))(lambda s=s: out_copy(s).start())
        pl.when(away(s) == 0)(lambda s=s: out_here(s).start())

    for direction in (0, 1):
        @pl.when(relays(direction))
        def _(direction=direction):
            out_first(0, direction).wait_recv()
            out_second(direction).start()

    def wait_c2(o, carry):
        c2_copy(o).wait_recv()
        return carry

    lax.fori_loop(1, nz, wait_c2, 0)

    def c3_copy(o, t):
        return remote(
            heads.at[lax.rem(x + o, NX), pl.ds(t * half, half)], kv_hbm.at[c, x, :, :, :],
            c3_s.at[o, t], c3_r.at[c, x], at_x(o, t),
        )

    def c3_here():
        return pltpu.make_async_copy(heads.at[x, pl.ds(c * half, half)], kv_hbm.at[c, x, :, :, :], c3_l)

    for o in range(1, NX):
        for t in (0, 1):
            c3_copy(o, t).start()
    c3_copy(0, 1 - c).start()
    c3_here().start()

    for kind in (0, 1):
        for h in range(NX):
            @pl.when((kind != c) | (h != x))
            def _(kind=kind, h=h):
                remote(
                    heads.at[0, pl.ds(0, half)], kv_hbm.at[kind, h, :, :, :],
                    c3_s.at[0, 0], c3_r.at[kind, h], sibling,
                ).wait_recv()

    c3_here().wait()
    c3_copy(0, 1 - c).wait_send()
    for o in range(1, NX):
        for t in (0, 1):
            c3_copy(o, t).wait_send()
    for i in (0, 1):
        @pl.when(2 * c + i != x)
        def _(i=i):
            cols = pl.ds(i * width, width)
            remote(obuf.at[0], out_hbm.at[:, cols], out_s.at[0, 0], out_r.at[i], sibling).wait_recv()

    for s in (0, 1):
        @pl.when(away(s) == 2)
        def _(s=s):
            for direction in (0, 1):
                out_first(s, direction).wait_send()

        pl.when((away(s) == 1) | (away(s) == 3))(lambda s=s: out_copy(s).wait_send())
        pl.when(away(s) == 0)(lambda s=s: out_here(s).wait())
        pl.when(relays(s))(lambda s=s: out_second(s).wait_send())
        for direction in (0, 1):
            a_send(s, direction).wait_send()
        a_forward(s).wait_send()
    for b in (0, 1):
        @pl.when(2 * c + b != x)
        def _(b=b):
            for copy in w0(b):
                copy.wait_send()

    for o in range(1, NX):
        meta_copy(o).wait_send()

    @pl.when(is_source)
    def _():
        for i in range(4):
            for direction in (0, 1):
                x_send(direction, i).wait_send()

    for s in (0, 1):
        for i in (0, 1):
            pl.when(away(s) == 1)(lambda s=s, i=i: x_forward(s, i, 0).wait_send())
            pl.when(away(s) == 3)(lambda s=s, i=i: x_forward(s, 2 + i, 1).wait_send())
        own_to_sibling(s).wait_send()
        swapped(s).wait_send()
    o_own_sibling().wait_send()

    def drain_z(o, carry):
        d_copy(o).wait_send()
        c1_copy(o).wait_send()
        c2_copy(o).wait_send()
        return carry

    lax.fori_loop(1, nz, drain_z, 0)

    def drain_ring(idx, carry):
        hop(0, z, idx, 0).wait_send()
        hop(0, z, idx, 1).wait_send()
        to_sibling(z, idx).wait_send()
        to_partner(z, idx).wait_send()
        y_to_sibling(z, idx).wait_send()
        o_hop(0, z, idx).wait_send()
        o_partner(z, idx).wait_send()
        o_y_sibling(z, idx).wait_send()
        o_sibling(z, idx).wait_send()
        return carry

    lax.fori_loop(0, last + 1, drain_ring, 0)


def on_device(normed, q_weight, kv_weight, o_weight, lengths, destinations):
    tokens = normed[0]
    total, width = tokens.shape
    nz = lax.axis_size("dp") // NX
    rows = q_weight.shape[0]
    q_cols = q_weight.shape[1] // 2
    kv_rows = kv_weight.reshape(rows, -1)
    o_t = o_weight.T
    cosine, sine = tables(total)
    columns = q_cols + 2 * HD
    o_cols = rows * nz
    piece = total // nz
    hops = nz - 1
    bf16, f32 = jnp.bfloat16, jnp.float32
    dma = pltpu.SemaphoreType.DMA
    scratch = [
        pltpu.VMEM((width, columns), bf16),
        pltpu.VMEM((2, o_cols, o_weight.shape[0]), bf16),
        pltpu.VMEM((2, total, width), bf16),
        pltpu.VMEM((2, NX, total, q_cols), bf16),
        pltpu.VMEM((2, total, columns), f32),
        pltpu.VMEM((2, total, o_cols), f32),
        pltpu.VMEM((2, total, o_cols), bf16),
        pltpu.VMEM((NX, 2, HD), jnp.int32),
        pltpu.VMEM((nz, 1, HD), jnp.int32),
        pltpu.VMEM((1, HD), jnp.int32),
        pltpu.SMEM((1, HD), jnp.int32),
        pltpu.VMEM((NX, total, HD), bf16),
        pltpu.VMEM((2, total, HD), bf16),
        pltpu.VMEM((NX * nz, piece, HD), bf16),
        pltpu.VMEM((NX, nz, piece, HD), bf16),
        pltpu.VMEM((NX, nz, piece, HD), bf16),
    ]
    shapes = [
        (NX,), (NX,), (2, 3), (2,), (hops, 2), (hops, 2), (hops,), (hops,), (hops,), (hops,), (hops,), (hops,), (2,), (2,),
        (hops,), (hops,), (hops,), (hops,), None, None, None, (2, 4), (2, 2), (2, 4), (2, 2), (2,), (2, 3), (2,), (2,),
        (nz,), (nz,), (nz,), (nz,), None, (nz,), (nz,), (NX, 2), (2, NX), None, (2, 2), (2,), None,
    ]
    scratch += [dma if shape is None else dma(shape) for shape in shapes]
    scratch.append(pltpu.SemaphoreType.REGULAR((2,)))
    scratch += [pltpu.VMEM((2, 2, total, HD), bf16), pltpu.VMEM((2, total // 2, o_cols), bf16), dma((2,)), dma((2,))]
    scratch += [dma((hops,))] * 4
    smem = pl.BlockSpec(memory_space=pltpu.SMEM)
    vmem = pl.BlockSpec(memory_space=pltpu.VMEM)
    any_space = pl.BlockSpec(memory_space=pl.ANY)
    projected, cache = pl.pallas_call(
        functools.partial(kernel, nz),
        out_shape=(
            jax.ShapeDtypeStruct((total, 2 * o_cols), bf16),
            jax.ShapeDtypeStruct((2, NX, nz // 2, piece, HD), bf16),
        ),
        in_specs=[any_space, vmem, vmem, vmem, vmem, vmem, smem, smem],
        out_specs=(any_space, any_space),
        scratch_shapes=scratch,
        compiler_params=pltpu.CompilerParams(
            collective_id=0, has_side_effects=True, vmem_limit_bytes=60 * 1024 * 1024
        ),
    )(tokens, q_weight, kv_rows, o_t, cosine, sine, destinations, lengths)
    return (projected[None], cache.reshape(1, 2, NX, total // 2, HD))


def solution(mesh):
    placed = (
        P(("parts", "dp"), None, None),
        P("dp", "tensor"),
        P("dp", None, "tensor"),
        P("tensor", "dp"),
        P(("parts", "dp")),
        P(("parts", "dp")),
    )
    return jax.shard_map(
        on_device,
        mesh=mesh,
        in_specs=placed,
        out_specs=(
            P(("parts", "dp"), None, "tensor"),
            P(("parts", "dp"), None, None, "tensor", None),
        ),
        check_vma=False,
    )
```

time: 133 us -> 129 us (0.970); the launches traced: 130 us -> 129 us
  other arithmetic: 2.04 us -> 0 us
    concatenate x2 -> x0, other arithmetic: 1.53 us -> none  [the longest x1 0.84 us: tables(): jnp.concatenate([cosine, cosine], axis=-1)]
    unnamed x6 -> x5, local copies, waits for them, and re-layouts: 3.06 us -> 4.53 us
where the time goes in v2:
time: 129 us
  Pallas kernels  122 us (95%)
  local copies, waits for them, and re-layouts  4.53 us (4%)
  between operations  1.94 us (2%)
    pallas_call x1, Pallas kernels, on_device(): pl.pallas_call(functools.partial(kernel, nz), out_shape=(jax.ShapeDtypeSt...  122 us
    unnamed x5, local copies, waits for them, and re-layouts  4.53 us

profile of v2, /device:TPU:33, one launch (start us, length us, event | category | flops | bytes accessed | tf_op | source)
XLA Modules:
  0.0 128.9 jit_solution(13840810334929215252)
XLA Ops:
  1.9 1.5 %copy.10 = bf16[8,8,2,256]{3,1,2,0:T(8,128)(2,1)} copy(bf16[8,8,2,256]{3,2,1,0:T(2,128)(2,1)} %bitcast.11) | data formatting | bytes 131072
  3.4 122.4 %shard_map.95 = (bf16[256,2048]{1,0:T(8,128)(2,1)}, bf16[2,4,8,16,128]{4,3,2,1,0:T(8,128)(2,1)}) custom-call(bf16[256,4096]{1,0:T(8,128)(2,1)} %bitcast.6, bf16[64,1024]{1,0:T(8,128)(2,1)} %q_ref.1, bf16[64,512]{1,0:T(8,128)(2,1)} %bitcast.8, bf16[64,1024]{1,0:T(8,128)(2,1)} %bitcast.10, f32[256,128]{1,0:T(8,128)} %constant.4.clone.cos_ref, ...), custom_call_target="tpu_custom_call" | custom-call | tf_op jit(solution)/shard_map/pallas_call | solution.py:758
  125.8 0.0 copy-start
  125.8 2.3 %copy.15 = bf16[1,256,2048]{2,1,0:T(8,128)(2,1)} copy(bf16[1,256,2048]{2,1,0:T(8,128)(2,1)} %bitcast.7) | data formatting | bytes 2097152
  128.2 0.0 copy-done
  128.2 0.7 copy.16
Async XLA Ops:
  125.8 2.4 %copy-start = (bf16[2,4,8,16,128]{4,3,2,1,0:T(8,128)(2,1)S(1)}, bf16[2,4,8,16,128]{4,3,2,1,0:T(8,128)(2,1)}, u32[]{:S(2)}) copy-start(bf16[2,4,8,16,128]{4,3,2,1,0:T(8,128)(2,1)} %get-tuple-element.5) | copy-start | bytes 786436

commit v3 on v2

--- a/solution.py
+++ b/solution.py
@@ -12,9 +12,10 @@
 HD = 128
 ROPE_BASE = 500000.0
 NX = 4
-KC = 512
+KC = 1024
 QC = 64
 LAG = 1
+Y_LAG = 3
 
 
 def tables(total):
@@ -43,7 +44,7 @@
 def kernel(
     nz, x_hbm, q_ref, kv_ref, o_t, cos_ref, sin_ref, dest_ref, length_ref, out_hbm, kv_hbm,
     wbuf, wobuf, xbuf, att, acc, oacc, obuf, meta, dests, srcv, srcs, kvall, swap, spread, perm, heads,
-    meta_s, meta_r, w0_s, w0_r, ring_s, ring_r, sib_s, sib_r, y_s, y_r, ysib_s, ysib_r, own_s, own_r,
+    meta_s, meta_r, w0_s, w0_r, ring_s, ring_r, sib_s, sib_r, y_s, y_r, own_s, own_r,
     o_s, o_r, osib_s, osib_r, oown_s, oown_r, x_l, x_s, xf_s, x_r, a_s, af_s, a_r, swap_s, swap_r,
     dest_s, dest_r, c1_s, c1_r, src_l, c2_s, c2_r, c3_s, c3_r, c3_l, out_s, out_r, out_l, ready, kvbuf, relay, relay_s, relay_r,
     oy_s, oy_r, oysib_s, oysib_r,
@@ -84,11 +85,11 @@
     pl.when(z != 1)(lambda: greet(ready.at[0], at_z(down, c)))
     pl.when(z == 0)(lambda: greet(ready.at[1], at_z(up, c)))
 
-    columns = wbuf.shape[1]
+    columns = wbuf.shape[2]
     q_cols = columns - 2 * HD
 
     def w_block(xs, zs):
-        return wbuf.at[pl.ds(pl.multiple_of((xs * nz + zs) * rows, rows), rows), :]
+        return wbuf.at[xs, pl.ds(pl.multiple_of(zs * rows, rows), rows), :]
 
     def w0_parts(b):
         return (
@@ -179,37 +180,35 @@
                 x_forward(s, 2 + i, 1).wait_recv()
                 x_forward(s, 2 + i, 1).start()
 
-    def hop(direction, zs, idx, part_of):
-        first_row = ((2 * c + yb) * nz + zs) * rows + part_of * (rows // 2)
-        blk = wbuf.at[pl.ds(pl.multiple_of(first_row, rows // 2), rows // 2), :]
-        return remote(
-            blk, blk, ring_s.at[idx, part_of], ring_r.at[idx, part_of],
+    def w_part(zs, core, which):
+        cols = pl.ds(q_cols, 2 * HD)
+        if which:
+            at = yb if which == 1 else 1 - yb
+            cols = pl.ds(pl.multiple_of(at * (q_cols // 2), q_cols // 2), q_cols // 2)
+        return wbuf.at[pl.ds(2 * core, 2), pl.ds(pl.multiple_of(zs * rows, rows), rows), cols]
+
+    def hop(direction, zs, idx, which):
+        blk = w_part(zs, c, which)
+        return remote(
+            blk, blk, ring_s.at[idx, which], ring_r.at[idx, which],
             at_z(up if direction == 0 else down, c),
         )
 
-    def to_sibling(zs, idx):
-        blk = w_block(2 * c + yb, zs)
-        return remote(blk, blk, sib_s.at[idx], sib_r.at[idx], sibling)
-
-    def from_sibling(zs, idx):
-        blk = w_block(2 * (1 - c) + yb, zs)
-        return remote(blk, blk, sib_s.at[idx], sib_r.at[idx], sibling)
+    def to_sibling(zs, idx, which):
+        blk = w_part(zs, c, which)
+        return remote(blk, blk, sib_s.at[idx, which], sib_r.at[idx, which], sibling)
 
     def to_partner(zs, idx):
-        blk = w_block(2 * c + yb, zs)
+        blk = w_part(zs, c, 1)
         return remote(blk, blk, y_s.at[idx], y_r.at[idx], partner)
 
     def from_partner(zs, idx):
-        blk = w_block(2 * c + 1 - yb, zs)
+        blk = w_part(zs, c, 2)
         return remote(blk, blk, y_s.at[idx], y_r.at[idx], partner)
 
-    def y_to_sibling(zs, idx):
-        blk = w_block(2 * c + 1 - yb, zs)
-        return remote(blk, blk, ysib_s.at[idx], ysib_r.at[idx], sibling)
-
-    def own_to_sibling(i):
-        blk = w_block(2 * c + i, z)
-        return remote(blk, blk, own_s.at[i], own_r.at[i], sibling)
+    def own_to_sibling():
+        blk = wbuf.at[pl.ds(2 * c, 2), pl.ds(pl.multiple_of(z * rows, rows), rows), :]
+        return remote(blk, blk, own_s, own_r, sibling)
 
     def o_block(zs, core):
         return wobuf.at[core, pl.ds(pl.multiple_of(zs * QC, QC), QC), :]
@@ -247,8 +246,7 @@
             remote(blk, blk, w0_s.at[0, 0], w0_r.at[i], sibling).wait_recv()
 
     first = (0, half - 1)
-    for i in (0, 1):
-        own_to_sibling(i).start()
+    own_to_sibling().start()
     pl.when(z != 0)(lambda: pl.semaphore_wait(ready.at[0], 1))
     for h in (0, 1):
         hop(0, z, first[0], h).start()
@@ -266,7 +264,7 @@
     def partner_on(direction, k, idx):
         zs = block_of(direction, k)
         from_partner(zs, idx).wait_recv()
-        y_to_sibling(zs, idx).start()
+        to_sibling(zs, idx, 2).start()
 
     def w_half(direction, k, h):
         idx = slot_of(direction, k)
@@ -280,7 +278,8 @@
     def w_rest(direction, k):
         idx = slot_of(direction, k)
         zs = block_of(direction, k)
-        to_sibling(zs, idx).start()
+        to_sibling(zs, idx, 0).start()
+        to_sibling(zs, idx, 1).start()
         to_partner(zs, idx).start()
 
     def o_step(k):
@@ -294,6 +293,8 @@
                 o_hop(direction, zs, jnp.where(k == half - 1, last, idx + 1)).start()
 
             o_sibling(zs, idx).start()
+            if direction == 0:
+                o_partner(zs, idx).start()
 
     def ring_step(k, carry):
         for h in (0, 1):
@@ -305,10 +306,10 @@
         def _():
             o_step(k - LAG)
 
-        @pl.when(k > 1)
+        @pl.when(k > Y_LAG)
         def _():
             for direction in (0, 1):
-                partner_on(direction, k - 1, slot_of(direction, k - 1))
+                partner_on(direction, k - Y_LAG, slot_of(direction, k - Y_LAG))
 
         return carry
 
@@ -321,31 +322,17 @@
     pass_on(1)
     lax.fori_loop(5, half, ring_step, 0)
     far = block_of(0, half)
-    for h in (0, 1):
-        hop(0, far, last, h).wait_recv()
-    to_sibling(far, last).start()
+    for which in (0, 1):
+        hop(0, far, last, which).wait_recv()
+        to_sibling(far, last, which).start()
     to_partner(far, last).start()
-    for direction in (0, 1):
-        partner_on(direction, half - 1, slot_of(direction, half - 1))
-    for k in range(half - LAG, half):
-        o_step(k)
-    for direction in (0, 1):
-        def o_over(k, carry, direction=direction):
-            o_partner(block_of(direction, k), slot_of(direction, k)).start()
-            return carry
-
-        lax.fori_loop(1, half, o_over, 0)
-    from_partner(far, last).wait_recv()
-    y_to_sibling(far, last).start()
 
     def arrived(idx, carry):
-        from_sibling(z, idx).wait_recv()
-        remote(w_block(2 * c, z), w_block(2 * c, z), ysib_s.at[idx], ysib_r.at[idx], sibling).wait_recv()
+        to_sibling(z, idx, 0).wait_recv()
         return carry
 
     lax.fori_loop(0, last + 1, arrived, 0)
-    for i in (0, 1):
-        own_to_sibling(i).wait_recv()
+    own_to_sibling().wait_recv()
     for o in range(1, NX):
         meta_copy(o).wait_recv()
 
@@ -371,9 +358,19 @@
             at_x(1 if direction == 0 else -1, c),
         )
 
-    def a_forward(s):
-        blk = att.at[s, lax.rem(x + (NX - 1 if s == 0 else 1), NX)]
-        return remote(blk, blk, af_s.at[s], a_r.at[s, 2], at_x(1 if s == 0 else -1, c))
+    def a_forward(s, direction):
+        source = lax.rem(x + (NX - 1 if direction == 0 else 1), NX)
+        blk = att.at[s, source, pl.ds(direction * (total // 2), total // 2)]
+        return remote(
+            blk, blk, af_s.at[s, direction], a_r.at[s, 2 + direction],
+            at_x(1 if direction == 0 else -1, c),
+        )
+
+    def pass_attended(s):
+        for direction in (0, 1):
+            a_send(s, direction).wait_recv()
+        for direction in (0, 1):
+            a_forward(s, direction).start()
 
     def x_wait(s):
         @pl.when(away(s) == 0)
@@ -390,18 +387,25 @@
             for q in (0, 1):
                 x_arrival(s, q).wait_recv()
 
-    def project(s, start, size):
+    def project(start, size):
         cols = pl.ds(start, size)
-        acc[s, :, cols] = jnp.zeros((total, size), jnp.float32)
-
-        def part_of(i, carry):
+        per = nz * rows // KC
+
+        def part_of(i):
             deep = pl.ds(pl.multiple_of(i * KC, KC), KC)
-            acc[s, :, cols] += jnp.dot(
-                xbuf[s, :, deep], wbuf[deep, cols], preferred_element_type=jnp.float32
-            )
+            inside = pl.ds(pl.multiple_of(lax.rem(i, per) * KC, KC), KC)
+            both = xbuf[:, :, deep].reshape(2 * total, KC)
+            return jnp.dot(
+                both, wbuf[lax.div(i, per), inside, cols], preferred_element_type=jnp.float32
+            ).reshape(2, total, size)
+
+        acc[:, :, cols] = part_of(0)
+
+        def add(i, carry):
+            acc[:, :, cols] += part_of(i)
             return carry
 
-        lax.fori_loop(0, wbuf.shape[0] // KC, part_of, 0)
+        lax.fori_loop(1, xbuf.shape[2] // KC, add, 0)
 
     def cache_rows(s):
         length = meta[2 * c + s, pl.ds(1, 1), :]
@@ -465,28 +469,42 @@
         c1_copy(o).start()
         return carry
 
-    apart = away(0)
-    near = jnp.where((apart == 1) | (apart == 2), 1, 0)
     lax.fori_loop(1, nz, send_dest, 0)
-    for s in (near, 1 - near):
+    for s in (0, 1):
         x_wait(s)
-        project(s, q_cols, 2 * HD)
+    project(q_cols, 2 * HD)
+    for s in (0, 1):
         cache_rows(s)
         swapped(s).start()
-    o_hop(0, far, last).wait_recv()
-    o_sibling(far, last).start()
-    o_partner(far, last).start()
+    for k in range(half - LAG, half):
+        o_step(k)
+    def o_over(k, carry):
+        o_partner(block_of(1, k), slot_of(1, k)).start()
+        return carry
+
+    lax.fori_loop(1, half, o_over, 0)
+
+    for k in range(half - Y_LAG, half):
+        for direction in (0, 1):
+            partner_on(direction, k, slot_of(direction, k))
+    partner_on(0, half, last)
     for s in (0, 1):
         swapped(s).wait_recv()
     lax.fori_loop(1, nz, send_c1, 0)
     spread[pl.ds(z * NX, NX)] = kvall[:, pl.ds(pl.multiple_of(z * piece, piece), piece), :]
-    project(near, 0, q_cols)
-    attend(near)
-    project(1 - near, 0, q_cols)
-    attend(1 - near)
-    for s in (0, 1):
-        a_send(s, s).wait_recv()
-        a_forward(s).start()
+    def q_arrived(idx, carry):
+        to_sibling(z, idx, 1).wait_recv()
+        to_sibling(z, idx, 2).wait_recv()
+        return carry
+
+    lax.fori_loop(0, last + 1, q_arrived, 0)
+    project(0, q_cols)
+    o_hop(0, far, last).wait_recv()
+    o_sibling(far, last).start()
+    o_partner(far, last).start()
+    attend(0)
+    attend(1)
+    pass_attended(0)
     def d_wait(o, carry):
         d_copy(o).wait_recv()
         c1_copy(o).wait_recv()
@@ -506,10 +524,11 @@
     to_scalars.wait()
 
     def reorder(d, carry):
-        perm[lax.div(d, nz), lax.rem(d, nz)] = spread[srcs[0, d]]
-        return carry
-
-    lax.fori_loop(0, NX * nz, reorder, 0)
+        for j in range(NX):
+            perm[j, d] = spread[srcs[0, j * nz + d]]
+        return carry
+
+    lax.fori_loop(0, nz, reorder, 0, unroll=4)
 
     def c2_copy(o):
         to = lax.rem(z + o, nz)
@@ -521,7 +540,6 @@
 
     lax.fori_loop(1, nz, send_c2, 0)
     heads[:, z] = perm[:, z]
-
     def o_crossed(idx, carry):
         zs = jnp.where(
             idx == last, far,
@@ -534,6 +552,7 @@
 
     lax.fori_loop(0, last + 1, o_crossed, 0)
 
+    pass_attended(1)
     def o_arrived(idx, carry):
         o_sibling(z, idx).wait_recv()
         o_y_sibling(z, idx).wait_recv()
@@ -552,9 +571,6 @@
 
     for s in (0, 1):
         oacc[s] = head_rows(s, x)
-    for s in (0, 1):
-        a_send(s, 1 - s).wait_recv()
-    for s in (0, 1):
         for direction in (0, 1):
             oacc[s] += head_rows(s, lax.rem(x + (NX - 1 if direction == 0 else 1), NX))
 
@@ -594,7 +610,8 @@
         return lax.div(to, 2) == c
 
     for s in (0, 1):
-        a_forward(s).wait_recv()
+        for direction in (0, 1):
+            a_forward(s, direction).wait_recv()
         obuf[s] = (oacc[s] + head_rows(s, lax.rem(x + 2, NX))).astype(jnp.bfloat16)
 
         @pl.when(away(s) == 2)
@@ -663,7 +680,8 @@
         pl.when(relays(s))(lambda s=s: out_second(s).wait_send())
         for direction in (0, 1):
             a_send(s, direction).wait_send()
-        a_forward(s).wait_send()
+        for direction in (0, 1):
+            a_forward(s, direction).wait_send()
     for b in (0, 1):
         @pl.when(2 * c + b != x)
         def _(b=b):
@@ -683,8 +701,8 @@
         for i in (0, 1):
             pl.when(away(s) == 1)(lambda s=s, i=i: x_forward(s, i, 0).wait_send())
             pl.when(away(s) == 3)(lambda s=s, i=i: x_forward(s, 2 + i, 1).wait_send())
-        own_to_sibling(s).wait_send()
         swapped(s).wait_send()
+    own_to_sibling().wait_send()
     o_own_sibling().wait_send()
 
     def drain_z(o, carry):
@@ -698,9 +716,9 @@
     def drain_ring(idx, carry):
         hop(0, z, idx, 0).wait_send()
         hop(0, z, idx, 1).wait_send()
-        to_sibling(z, idx).wait_send()
+        for which in (0, 1, 2):
+            to_sibling(z, idx, which).wait_send()
         to_partner(z, idx).wait_send()
-        y_to_sibling(z, idx).wait_send()
         o_hop(0, z, idx).wait_send()
         o_partner(z, idx).wait_send()
         o_y_sibling(z, idx).wait_send()
@@ -726,7 +744,7 @@
     bf16, f32 = jnp.bfloat16, jnp.float32
     dma = pltpu.SemaphoreType.DMA
     scratch = [
-        pltpu.VMEM((width, columns), bf16),
+        pltpu.VMEM((NX, width // NX, columns), bf16),
         pltpu.VMEM((2, o_cols, o_weight.shape[0]), bf16),
         pltpu.VMEM((2, total, width), bf16),
         pltpu.VMEM((2, NX, total, q_cols), bf16),
@@ -744,8 +762,8 @@
         pltpu.VMEM((NX, nz, piece, HD), bf16),
     ]
     shapes = [
-        (NX,), (NX,), (2, 3), (2,), (hops, 2), (hops, 2), (hops,), (hops,), (hops,), (hops,), (hops,), (hops,), (2,), (2,),
-        (hops,), (hops,), (hops,), (hops,), None, None, None, (2, 4), (2, 2), (2, 4), (2, 2), (2,), (2, 3), (2,), (2,),
+        (NX,), (NX,), (2, 3), (2,), (hops, 2), (hops, 2), (hops, 3), (hops, 3), (hops,), (hops,), None, None,
+        (hops,), (hops,), (hops,), (hops,), None, None, None, (2, 4), (2, 2), (2, 4), (2, 2), (2, 2), (2, 4), (2,), (2,),
         (nz,), (nz,), (nz,), (nz,), None, (nz,), (nz,), (NX, 2), (2, NX), None, (2, 2), (2,), None,
     ]
     scratch += [dma if shape is None else dma(shape) for shape in shapes]
@@ -758,11 +776,11 @@
     projected, cache = pl.pallas_call(
         functools.partial(kernel, nz),
         out_shape=(
-            jax.ShapeDtypeStruct((total, 2 * o_cols), bf16),
-            jax.ShapeDtypeStruct((2, NX, nz // 2, piece, HD), bf16),
+            pltpu.VMEM((total, 2 * o_cols), bf16),
+            pltpu.VMEM((2, NX, nz // 2, piece, HD), bf16),
         ),
         in_specs=[any_space, vmem, vmem, vmem, vmem, vmem, smem, smem],
-        out_specs=(any_space, any_space),
+        out_specs=(vmem, vmem),
         scratch_shapes=scratch,
         compiler_params=pltpu.CompilerParams(
             collective_id=0, has_side_effects=True, vmem_limit_bytes=60 * 1024 * 1024

time: 129 us -> 122 us (0.946)
  Pallas kernels: 122 us -> 117 us
  local copies, waits for them, and re-layouts: 4.53 us -> 3.15 us
    pallas_call x1, Pallas kernels: 122 us -> 117 us  [on_device(): pl.pallas_call(functools.partial(kernel, nz), out_shape=(pltpu.VMEM((tota...]
    unnamed x5 -> x3, local copies, waits for them, and re-layouts: 4.53 us -> 3.15 us
where the time goes in v3:
time: 122 us
  Pallas kernels  117 us (96%)
  local copies, waits for them, and re-layouts  3.15 us (3%)
  between operations  1.93 us (2%)
    pallas_call x1, Pallas kernels, on_device(): pl.pallas_call(functools.partial(kernel, nz), out_shape=(pltpu.VMEM((tota...  117 us
    unnamed x3, local copies, waits for them, and re-layouts  3.15 us

profile of v3, /device:TPU:33, one launch (start us, length us, event | category | flops | bytes accessed | tf_op | source)
XLA Modules:
  0.0 121.8 jit_solution(9357585286466201801)
XLA Ops:
  1.9 1.5 %copy.10 = bf16[8,8,2,256]{3,1,2,0:T(8,128)(2,1)} copy(bf16[8,8,2,256]{3,2,1,0:T(2,128)(2,1)} %bitcast.11) | data formatting | bytes 131072
  3.4 116.7 %shard_map.95 = (bf16[256,2048]{1,0:T(8,128)(2,1)S(1)}, bf16[2,4,8,16,128]{4,3,2,1,0:T(8,128)(2,1)S(1)}) custom-call(bf16[256,4096]{1,0:T(8,128)(2,1)} %bitcast.8, bf16[64,1024]{1,0:T(8,128)(2,1)} %q_ref.1, bf16[64,512]{1,0:T(8,128)(2,1)} %bitcast.9, bf16[64,1024]{1,0:T(8,128)(2,1)} %bitcast.10, f32[256,128]{1,0:T(8,128)} %constant.4.clone.cos_ref, ...), custom_call_target="tpu_custom_call" | custom-call | tf_op jit(solution)/shard_map/pallas_call | solution.py:776
  120.1 1.0 copy.13
  121.1 0.7 copy.14

commit v4 on v3

--- a/solution.py
+++ b/solution.py
@@ -42,12 +42,12 @@
 
 
 def kernel(
-    nz, x_hbm, q_ref, kv_ref, o_t, cos_ref, sin_ref, dest_ref, length_ref, out_hbm, kv_hbm,
+    nz, x_hbm, q_hbm, kv_rows, o_hbm, cos_hbm, sin_hbm, dest_ref, length_ref, out_hbm, kv_hbm,
     wbuf, wobuf, xbuf, att, acc, oacc, obuf, meta, dests, srcv, srcs, kvall, swap, spread, perm, heads,
     meta_s, meta_r, w0_s, w0_r, ring_s, ring_r, sib_s, sib_r, y_s, y_r, own_s, own_r,
     o_s, o_r, osib_s, osib_r, oown_s, oown_r, x_l, x_s, xf_s, x_r, a_s, af_s, a_r, swap_s, swap_r,
     dest_s, dest_r, c1_s, c1_r, src_l, c2_s, c2_r, c3_s, c3_r, c3_l, out_s, out_r, out_l, ready, kvbuf, relay, relay_s, relay_r,
-    oy_s, oy_r, oysib_s, oysib_r,
+    oy_s, oy_r, oysib_s, oysib_r, q_ref, kv_ref, o_t, cos_ref, sin_ref, load,
 ):
     part, dp, c = lax.axis_index("parts"), lax.axis_index("dp"), lax.axis_index("tensor")
     x, z = lax.div(dp, nz), lax.rem(dp, nz)
@@ -69,6 +69,15 @@
     partner = (mate, dp, c)
     up, down = lax.rem(z + 1, nz), lax.rem(z + nz - 1, nz)
 
+    loads = [
+        pltpu.make_async_copy(src, dst, load.at[i])
+        for i, (src, dst) in enumerate(
+            ((q_hbm, q_ref), (kv_rows, kv_ref), (o_hbm, o_t), (cos_hbm, cos_ref), (sin_hbm, sin_ref))
+        )
+    ]
+    for copy in loads:
+        copy.start()
+
     barrier = pltpu.get_barrier_semaphore()
 
     def greet(semaphore, device):
@@ -83,6 +92,8 @@
         barrier, len(greeted) + jnp.where(z == 1, 0, 1) + jnp.where(z == 0, 1, 0)
     )
     pl.when(z != 1)(lambda: greet(ready.at[0], at_z(down, c)))
+    for copy in loads:
+        copy.wait()
     pl.when(z == 0)(lambda: greet(ready.at[1], at_z(up, c)))
 
     columns = wbuf.shape[2]
@@ -190,21 +201,21 @@
     def hop(direction, zs, idx, which):
         blk = w_part(zs, c, which)
         return remote(
-            blk, blk, ring_s.at[idx, which], ring_r.at[idx, which],
+            blk, blk, ring_s, ring_r.at[idx, which],
             at_z(up if direction == 0 else down, c),
         )
 
     def to_sibling(zs, idx, which):
         blk = w_part(zs, c, which)
-        return remote(blk, blk, sib_s.at[idx, which], sib_r.at[idx, which], sibling)
+        return remote(blk, blk, sib_s, sib_r.at[which], sibling)
 
     def to_partner(zs, idx):
         blk = w_part(zs, c, 1)
-        return remote(blk, blk, y_s.at[idx], y_r.at[idx], partner)
+        return remote(blk, blk, y_s, y_r.at[idx], partner)
 
     def from_partner(zs, idx):
         blk = w_part(zs, c, 2)
-        return remote(blk, blk, y_s.at[idx], y_r.at[idx], partner)
+        return remote(blk, blk, y_s, y_r.at[idx], partner)
 
     def own_to_sibling():
         blk = wbuf.at[pl.ds(2 * c, 2), pl.ds(pl.multiple_of(z * rows, rows), rows), :]
@@ -220,21 +231,21 @@
     def o_hop(direction, zs, idx, src=None):
         blk = o_part(zs, yb)
         return remote(
-            blk if src is None else src, blk, o_s.at[idx], o_r.at[idx],
+            blk if src is None else src, blk, o_s, o_r.at[idx],
             at_z(up if direction == 0 else down, c),
         )
 
     def o_sibling(zs, idx):
         blk = o_part(zs, yb)
-        return remote(blk, blk, osib_s.at[idx], osib_r.at[idx], sibling)
+        return remote(blk, blk, osib_s, osib_r, sibling)
 
     def o_partner(zs, idx):
         blk = o_part(zs, yb)
-        return remote(blk, blk, oy_s.at[idx], oy_r.at[idx], partner)
+        return remote(blk, blk, oy_s, oy_r, partner)
 
     def o_y_sibling(zs, idx):
         blk = o_part(zs, 1 - yb)
-        return remote(blk, blk, oysib_s.at[idx], oysib_r.at[idx], sibling)
+        return remote(blk, blk, oysib_s, oysib_r, sibling)
 
     def o_own_sibling():
         return remote(o_t, o_block(z, c), oown_s, oown_r, sibling)
@@ -327,11 +338,11 @@
         to_sibling(far, last, which).start()
     to_partner(far, last).start()
 
-    def arrived(idx, carry):
-        to_sibling(z, idx, 0).wait_recv()
-        return carry
-
-    lax.fori_loop(0, last + 1, arrived, 0)
+    def w_all(start, size, semaphores):
+        blk = wbuf.at[pl.ds(0, 2), pl.ds(0, (nz - 1) * rows), pl.ds(start, size)]
+        return remote(blk, blk, *semaphores, sibling)
+
+    w_all(q_cols, 2 * HD, (sib_s, sib_r.at[0])).wait_recv()
     own_to_sibling().wait_recv()
     for o in range(1, NX):
         meta_copy(o).wait_recv()
@@ -451,14 +462,14 @@
         return remote(swap.at[s], kvall.at[2 * c + s], swap_s.at[s], swap_r.at[s], sibling)
 
     def d_copy(o):
-        return remote(dests.at[z], dests.at[z], dest_s.at[o], dest_r.at[o], at_z(lax.rem(z + o, nz), c))
+        return remote(dests.at[z], dests.at[z], dest_s, dest_r, at_z(lax.rem(z + o, nz), c))
 
     def c1_copy(o):
         to = lax.rem(z + o, nz)
         return remote(
             kvall.at[:, pl.ds(pl.multiple_of(to * piece, piece), piece), :],
             spread.at[pl.ds(z * NX, NX)],
-            c1_s.at[o], c1_r.at[o], at_z(to, c),
+            c1_s, c1_r, at_z(to, c),
         )
 
     def send_dest(o, carry):
@@ -492,12 +503,8 @@
         swapped(s).wait_recv()
     lax.fori_loop(1, nz, send_c1, 0)
     spread[pl.ds(z * NX, NX)] = kvall[:, pl.ds(pl.multiple_of(z * piece, piece), piece), :]
-    def q_arrived(idx, carry):
-        to_sibling(z, idx, 1).wait_recv()
-        to_sibling(z, idx, 2).wait_recv()
-        return carry
-
-    lax.fori_loop(0, last + 1, q_arrived, 0)
+    for which in (1, 2):
+        w_all(0, q_cols // 2, (sib_s, sib_r.at[which])).wait_recv()
     project(0, q_cols)
     o_hop(0, far, last).wait_recv()
     o_sibling(far, last).start()
@@ -505,12 +512,16 @@
     attend(0)
     attend(1)
     pass_attended(0)
-    def d_wait(o, carry):
-        d_copy(o).wait_recv()
-        c1_copy(o).wait_recv()
-        return carry
-
-    lax.fori_loop(1, nz, d_wait, 0)
+    def d_all():
+        blk = dests.at[pl.ds(0, nz - 1)]
+        return remote(blk, blk, dest_s, dest_r, sibling)
+
+    def c1_all():
+        blk = spread.at[pl.ds(0, NX * (nz - 1))]
+        return remote(blk, blk, c1_s, c1_r, sibling)
+
+    d_all().wait_recv()
+    c1_all().wait_recv()
     all_dests = dests[...].reshape(nz, HD)
     lanes = lax.broadcasted_iota(jnp.int32, (nz, HD), 1)
     prompt = lax.broadcasted_iota(jnp.int32, (nz, HD), 0) * NX
@@ -532,7 +543,7 @@
 
     def c2_copy(o):
         to = lax.rem(z + o, nz)
-        return remote(perm.at[:, to], heads.at[:, z], c2_s.at[o], c2_r.at[o], at_z(to, c))
+        return remote(perm.at[:, to], heads.at[:, z], c2_s, c2_r, at_z(to, c))
 
     def send_c2(o, carry):
         c2_copy(o).start()
@@ -540,25 +551,25 @@
 
     lax.fori_loop(1, nz, send_c2, 0)
     heads[:, z] = perm[:, z]
+    def o_all(semaphores):
+        blk = wobuf.at[c, pl.ds(0, (nz - 1) * (QC // 2)), :]
+        return remote(blk, blk, *semaphores, sibling)
+
+    o_all((oy_s, oy_r)).wait_recv()
+
     def o_crossed(idx, carry):
         zs = jnp.where(
             idx == last, far,
             jnp.where(idx < half - 1, block_of(0, idx + 1), block_of(1, idx + 2 - half)),
         )
-        o_part_y = o_part(zs, 1 - yb)
-        remote(o_part_y, o_part_y, oy_s.at[idx], oy_r.at[idx], partner).wait_recv()
         o_y_sibling(zs, idx).start()
         return carry
 
     lax.fori_loop(0, last + 1, o_crossed, 0)
 
     pass_attended(1)
-    def o_arrived(idx, carry):
-        o_sibling(z, idx).wait_recv()
-        o_y_sibling(z, idx).wait_recv()
-        return carry
-
-    lax.fori_loop(0, last + 1, o_arrived, 0)
+    o_all((osib_s, osib_r)).wait_recv()
+    o_all((oysib_s, oysib_r)).wait_recv()
     o_own_sibling().wait_recv()
 
     def head_rows(s, xs):
@@ -628,16 +639,16 @@
             out_first(0, direction).wait_recv()
             out_second(direction).start()
 
-    def wait_c2(o, carry):
-        c2_copy(o).wait_recv()
-        return carry
-
-    lax.fori_loop(1, nz, wait_c2, 0)
+    def c2_all():
+        blk = heads.at[:, pl.ds(0, nz - 1)]
+        return remote(blk, blk, c2_s, c2_r, sibling)
+
+    c2_all().wait_recv()
 
     def c3_copy(o, t):
         return remote(
             heads.at[lax.rem(x + o, NX), pl.ds(t * half, half)], kv_hbm.at[c, x, :, :, :],
-            c3_s.at[o, t], c3_r.at[c, x], at_x(o, t),
+            c3_s, c3_r, at_x(o, t),
         )
 
     def c3_here():
@@ -649,20 +660,13 @@
     c3_copy(0, 1 - c).start()
     c3_here().start()
 
-    for kind in (0, 1):
-        for h in range(NX):
-            @pl.when((kind != c) | (h != x))
-            def _(kind=kind, h=h):
-                remote(
-                    heads.at[0, pl.ds(0, half)], kv_hbm.at[kind, h, :, :, :],
-                    c3_s.at[0, 0], c3_r.at[kind, h], sibling,
-                ).wait_recv()
-
+    def c3_all():
+        blk = heads.at[:, pl.ds(0, (2 * NX - 1) * half // NX)]
+        return remote(blk, blk, c3_s, c3_r, sibling)
+
+    c3_all().wait_recv()
     c3_here().wait()
-    c3_copy(0, 1 - c).wait_send()
-    for o in range(1, NX):
-        for t in (0, 1):
-            c3_copy(o, t).wait_send()
+    c3_all().wait_send()
     for i in (0, 1):
         @pl.when(2 * c + i != x)
         def _(i=i):
@@ -705,27 +709,13 @@
     own_to_sibling().wait_send()
     o_own_sibling().wait_send()
 
-    def drain_z(o, carry):
-        d_copy(o).wait_send()
-        c1_copy(o).wait_send()
-        c2_copy(o).wait_send()
-        return carry
-
-    lax.fori_loop(1, nz, drain_z, 0)
-
-    def drain_ring(idx, carry):
-        hop(0, z, idx, 0).wait_send()
-        hop(0, z, idx, 1).wait_send()
-        for which in (0, 1, 2):
-            to_sibling(z, idx, which).wait_send()
-        to_partner(z, idx).wait_send()
-        o_hop(0, z, idx).wait_send()
-        o_partner(z, idx).wait_send()
-        o_y_sibling(z, idx).wait_send()
-        o_sibling(z, idx).wait_send()
-        return carry
-
-    lax.fori_loop(0, last + 1, drain_ring, 0)
+    for sent in (d_all(), c1_all(), c2_all()):
+        sent.wait_send()
+    w_all(0, q_cols, (ring_s, ring_r.at[0, 0])).wait_send()
+    w_all(0, columns, (sib_s, sib_r.at[0])).wait_send()
+    w_all(0, q_cols // 2, (y_s, y_r.at[0])).wait_send()
+    for pair in ((o_s, o_r.at[0]), (osib_s, osib_r), (oy_s, oy_r), (oysib_s, oysib_r)):
+        o_all(pair).wait_send()
 
 
 def on_device(normed, q_weight, kv_weight, o_weight, lengths, destinations):
@@ -762,14 +752,15 @@
         pltpu.VMEM((NX, nz, piece, HD), bf16),
     ]
     shapes = [
-        (NX,), (NX,), (2, 3), (2,), (hops, 2), (hops, 2), (hops, 3), (hops, 3), (hops,), (hops,), None, None,
-        (hops,), (hops,), (hops,), (hops,), None, None, None, (2, 4), (2, 2), (2, 4), (2, 2), (2, 2), (2, 4), (2,), (2,),
-        (nz,), (nz,), (nz,), (nz,), None, (nz,), (nz,), (NX, 2), (2, NX), None, (2, 2), (2,), None,
+        (NX,), (NX,), (2, 3), (2,), None, (hops, 2), None, (3,), None, (hops,), None, None,
+        None, (hops,), None, None, None, None, None, (2, 4), (2, 2), (2, 4), (2, 2), (2, 2), (2, 4), (2,), (2,),
+        None, None, None, None, None, None, None, None, None, None, (2, 2), (2,), None,
     ]
     scratch += [dma if shape is None else dma(shape) for shape in shapes]
     scratch.append(pltpu.SemaphoreType.REGULAR((2,)))
     scratch += [pltpu.VMEM((2, 2, total, HD), bf16), pltpu.VMEM((2, total // 2, o_cols), bf16), dma((2,)), dma((2,))]
-    scratch += [dma((hops,))] * 4
+    scratch += [dma] * 4
+    scratch += [pltpu.VMEM(a.shape, a.dtype) for a in (q_weight, kv_rows, o_t, cosine, sine)] + [dma((5,))]
     smem = pl.BlockSpec(memory_space=pltpu.SMEM)
     vmem = pl.BlockSpec(memory_space=pltpu.VMEM)
     any_space = pl.BlockSpec(memory_space=pl.ANY)
@@ -779,7 +770,7 @@
             pltpu.VMEM((total, 2 * o_cols), bf16),
             pltpu.VMEM((2, NX, nz // 2, piece, HD), bf16),
         ),
-        in_specs=[any_space, vmem, vmem, vmem, vmem, vmem, smem, smem],
+        in_specs=[any_space] * 6 + [smem, smem],
         out_specs=(vmem, vmem),
         scratch_shapes=scratch,
         compiler_params=pltpu.CompilerParams(

time: 122 us -> 117 us (0.959)
  Pallas kernels: 117 us -> 112 us
    pallas_call x1, Pallas kernels: 117 us -> 112 us  [on_device(): pl.pallas_call(functools.partial(kernel, nz), out_shape=(pltpu.VMEM((tota...]
where the time goes in v4:
time: 117 us
  Pallas kernels  112 us (96%)
  local copies, waits for them, and re-layouts  3.15 us (3%)
  between operations  1.93 us (2%)
    pallas_call x1, Pallas kernels, on_device(): pl.pallas_call(functools.partial(kernel, nz), out_shape=(pltpu.VMEM((tota...  112 us
    unnamed x3, local copies, waits for them, and re-layouts  3.15 us

profile of v4, /device:TPU:33, one launch (start us, length us, event | category | flops | bytes accessed | tf_op | source)
XLA Modules:
  0.0 117.1 jit_solution(15376511873429665842)
XLA Ops:
  1.9 1.5 %copy.10 = bf16[8,8,2,256]{3,1,2,0:T(8,128)(2,1)} copy(bf16[8,8,2,256]{3,2,1,0:T(2,128)(2,1)} %bitcast.11) | data formatting | bytes 131072
  3.4 112.0 %shard_map.95 = (bf16[256,2048]{1,0:T(8,128)(2,1)S(1)}, bf16[2,4,8,16,128]{4,3,2,1,0:T(8,128)(2,1)S(1)}) custom-call(bf16[256,4096]{1,0:T(8,128)(2,1)} %bitcast.8, bf16[64,1024]{1,0:T(8,128)(2,1)} %q_hbm.1, bf16[64,512]{1,0:T(8,128)(2,1)} %bitcast.9, bf16[64,1024]{1,0:T(8,128)(2,1)} %bitcast.10, f32[256,128]{1,0:T(8,128)} %constant.4.clone.cos_hbm, ...), custom_call_target="tpu_custom_call" | custom-call | tf_op jit(solution)/shard_map/pallas_call | solution.py:767
  115.4 1.0 copy.13
  116.4 0.7 copy.14

commit v5 on v4

--- a/solution.py
+++ b/solution.py
@@ -42,12 +42,12 @@
 
 
 def kernel(
-    nz, x_hbm, q_hbm, kv_rows, o_hbm, cos_hbm, sin_hbm, dest_ref, length_ref, out_hbm, kv_hbm,
+    nz, x_hbm, q_hbm, kv_hbm_in, o_hbm, cos_hbm, sin_hbm, dest_ref, length_ref, out_hbm, kv_hbm,
     wbuf, wobuf, xbuf, att, acc, oacc, obuf, meta, dests, srcv, srcs, kvall, swap, spread, perm, heads,
     meta_s, meta_r, w0_s, w0_r, ring_s, ring_r, sib_s, sib_r, y_s, y_r, own_s, own_r,
     o_s, o_r, osib_s, osib_r, oown_s, oown_r, x_l, x_s, xf_s, x_r, a_s, af_s, a_r, swap_s, swap_r,
     dest_s, dest_r, c1_s, c1_r, src_l, c2_s, c2_r, c3_s, c3_r, c3_l, out_s, out_r, out_l, ready, kvbuf, relay, relay_s, relay_r,
-    oy_s, oy_r, oysib_s, oysib_r, q_ref, kv_ref, o_t, cos_ref, sin_ref, load,
+    oy_s, oy_r, oysib_s, oysib_r, q_ref, kv_pair, kv_ref, o_t, cos_ref, sin_ref, load,
 ):
     part, dp, c = lax.axis_index("parts"), lax.axis_index("dp"), lax.axis_index("tensor")
     x, z = lax.div(dp, nz), lax.rem(dp, nz)
@@ -72,7 +72,7 @@
     loads = [
         pltpu.make_async_copy(src, dst, load.at[i])
         for i, (src, dst) in enumerate(
-            ((q_hbm, q_ref), (kv_rows, kv_ref), (o_hbm, o_t), (cos_hbm, cos_ref), (sin_hbm, sin_ref))
+            ((kv_hbm_in, kv_pair), (q_hbm, q_ref), (o_hbm, o_t), (cos_hbm, cos_ref), (sin_hbm, sin_ref))
         )
     ]
     for copy in loads:
@@ -88,11 +88,15 @@
         greet(barrier, device)
     pl.when(z != 0)(lambda: greet(barrier, at_z(up, c)))
     pl.when(z == 1)(lambda: greet(barrier, at_z(down, c)))
+    loads[0].wait()
+    pair = kv_pair[...].astype(jnp.float32)
+    for i in (0, 1):
+        kv_ref[:, 2 * HD * i : 2 * HD * (i + 1)] = pair[:, i, :].astype(jnp.bfloat16)
     pl.semaphore_wait(
         barrier, len(greeted) + jnp.where(z == 1, 0, 1) + jnp.where(z == 0, 1, 0)
     )
     pl.when(z != 1)(lambda: greet(ready.at[0], at_z(down, c)))
-    for copy in loads:
+    for copy in loads[1:]:
         copy.wait()
     pl.when(z == 0)(lambda: greet(ready.at[1], at_z(up, c)))
 
@@ -480,7 +484,6 @@
         c1_copy(o).start()
         return carry
 
-    lax.fori_loop(1, nz, send_dest, 0)
     for s in (0, 1):
         x_wait(s)
     project(q_cols, 2 * HD)
@@ -506,6 +509,7 @@
     for which in (1, 2):
         w_all(0, q_cols // 2, (sib_s, sib_r.at[which])).wait_recv()
     project(0, q_cols)
+    lax.fori_loop(1, nz, send_dest, 0)
     o_hop(0, far, last).wait_recv()
     o_sibling(far, last).start()
     o_partner(far, last).start()
@@ -724,7 +728,6 @@
     nz = lax.axis_size("dp") // NX
     rows = q_weight.shape[0]
     q_cols = q_weight.shape[1] // 2
-    kv_rows = kv_weight.reshape(rows, -1)
     o_t = o_weight.T
     cosine, sine = tables(total)
     columns = q_cols + 2 * HD
@@ -760,7 +763,8 @@
     scratch.append(pltpu.SemaphoreType.REGULAR((2,)))
     scratch += [pltpu.VMEM((2, 2, total, HD), bf16), pltpu.VMEM((2, total // 2, o_cols), bf16), dma((2,)), dma((2,))]
     scratch += [dma] * 4
-    scratch += [pltpu.VMEM(a.shape, a.dtype) for a in (q_weight, kv_rows, o_t, cosine, sine)] + [dma((5,))]
+    scratch += [pltpu.VMEM(a.shape, a.dtype) for a in (q_weight, kv_weight, kv_weight.reshape(rows, -1), o_t, cosine, sine)]
+    scratch.append(dma((5,)))
     smem = pl.BlockSpec(memory_space=pltpu.SMEM)
     vmem = pl.BlockSpec(memory_space=pltpu.VMEM)
     any_space = pl.BlockSpec(memory_space=pl.ANY)
@@ -776,7 +780,7 @@
         compiler_params=pltpu.CompilerParams(
             collective_id=0, has_side_effects=True, vmem_limit_bytes=60 * 1024 * 1024
         ),
-    )(tokens, q_weight, kv_rows, o_t, cosine, sine, destinations, lengths)
+    )(tokens, q_weight, kv_weight, o_t, cosine, sine, destinations, lengths)
     return (projected[None], cache.reshape(1, 2, NX, total // 2, HD))
 
 

time: 117 us -> 117 us (level)
  local copies, waits for them, and re-layouts: 3.15 us -> 1.67 us
    unnamed x3 -> x2, local copies, waits for them, and re-layouts: 3.15 us -> 1.67 us
where the time goes in v5:
time: 117 us
  Pallas kernels  113 us (97%)
  between operations  1.93 us (2%)
  local copies, waits for them, and re-layouts  1.67 us (1%)
    pallas_call x1, Pallas kernels, on_device(): pl.pallas_call(functools.partial(kernel, nz), out_shape=(pltpu.VMEM((tota...  113 us

profile of v5, /device:TPU:33, one launch (start us, length us, event | category | flops | bytes accessed | tf_op | source)
XLA Modules:
  0.0 116.7 jit_solution(12440441586300693631)
XLA Ops:
  1.9 113.1 %shard_map.95 = (bf16[256,2048]{1,0:T(8,128)(2,1)S(1)}, bf16[2,4,8,16,128]{4,3,2,1,0:T(8,128)(2,1)S(1)}) custom-call(bf16[256,4096]{1,0:T(8,128)(2,1)} %bitcast.6, bf16[64,1024]{1,0:T(8,128)(2,1)} %q_hbm.1, bf16[64,2,256]{2,1,0:T(2,128)(2,1)} %kv_hbm_in.1, bf16[64,1024]{1,0:T(8,128)(2,1)} %bitcast.7, f32[256,128]{1,0:T(8,128)} %constant.4.clone.cos_hbm, ...), custom_call_target="tpu_custom_call" | custom-call | tf_op jit(solution)/shard_map/pallas_call | solution.py:771
  115.0 1.0 copy.12
  116.0 0.7 copy.13

commit v6 on v5

--- a/solution.py
+++ b/solution.py
@@ -96,8 +96,7 @@
         barrier, len(greeted) + jnp.where(z == 1, 0, 1) + jnp.where(z == 0, 1, 0)
     )
     pl.when(z != 1)(lambda: greet(ready.at[0], at_z(down, c)))
-    for copy in loads[1:]:
-        copy.wait()
+    loads[1].wait()
     pl.when(z == 0)(lambda: greet(ready.at[1], at_z(up, c)))
 
     columns = wbuf.shape[2]
@@ -268,6 +267,7 @@
     pl.when(z == 1)(lambda: pl.semaphore_wait(ready.at[1], 1))
     for h in (0, 1):
         hop(1, z, first[1], h).start()
+    loads[2].wait()
     o_block(z, c)[...] = o_t[...]
 
     def block_of(direction, k):
@@ -357,6 +357,8 @@
         row = jnp.where(lane == j, meta[j, pl.ds(0, 1), :], row)
     dests[z] = row
 
+    for copy in loads[3:]:
+        copy.wait()
     cosine, sine = cos_ref[...], sin_ref[...]
 
     def rotated(u):

time: 117 us -> 117 us (level)
  no operation moved by 1% of the time
where the time goes in v6:
time: 117 us
  Pallas kernels  113 us (97%)
  between operations  1.93 us (2%)
  local copies, waits for them, and re-layouts  1.67 us (1%)
    pallas_call x1, Pallas kernels, on_device(): pl.pallas_call(functools.partial(kernel, nz), out_shape=(pltpu.VMEM((tota...  113 us

profile of v6, /device:TPU:33, one launch (start us, length us, event | category | flops | bytes accessed | tf_op | source)
XLA Modules:
  0.0 116.7 jit_solution(6872890042082686424)
XLA Ops:
  1.9 113.1 %shard_map.95 = (bf16[256,2048]{1,0:T(8,128)(2,1)S(1)}, bf16[2,4,8,16,128]{4,3,2,1,0:T(8,128)(2,1)S(1)}) custom-call(bf16[256,4096]{1,0:T(8,128)(2,1)} %bitcast.6, bf16[64,1024]{1,0:T(8,128)(2,1)} %q_hbm.1, bf16[64,2,256]{2,1,0:T(2,128)(2,1)} %kv_hbm_in.1, bf16[64,1024]{1,0:T(8,128)(2,1)} %bitcast.7, f32[256,128]{1,0:T(8,128)} %constant.4.clone.cos_hbm, ...), custom_call_target="tpu_custom_call" | custom-call | tf_op jit(solution)/shard_map/pallas_call | solution.py:773
  115.0 1.0 copy.12
  116.0 0.7 copy.13
